TPU v7x, 32 devices: a whole 2x2x4 slice. The times are simulated.
32 devices in a mesh: slab: 2 (over core), py: 4 (over z), pz: 4 (over y, x).
Axes of the slice: x: 2, y: 2, z: 4, core: 2. Of those that a mesh axis runs over, the one named last changes fastest.
Arguments:
- start_vector: float32 [32, 128, 256], P('pz', 'py', 'slab'), may hold values from -6 to 6
- potential: float32 [32, 128, 256], P('pz', 'py', 'slab'), may hold values from 0.5 to 4
Outputs:
- krylov_basis: float32 [6, 32, 128, 256], P(None, 'pz', 'py', 'slab')
- tridiagonal: float32 [2, 5], replicated
All inputs are finite; a program needn't handle non-finite values.
Results may differ from a plain program's by a relative error of at most 0.00012.
Values sent between devices are 32-bit elements; how exact they have to be, the bound alone decides.
A program may use at most 64 MiB of HBM per device.

v0:
```python
import functools

import jax
import jax.numpy as jnp
from jax import lax
from jax.experimental import pallas as pl
from jax.experimental.pallas import tpu as pltpu
from jax.sharding import PartitionSpec as P

ITERS = 5
EPSILON = 1e-06
DIAGONAL = 6.0
FIRST_SHIFTS = (3.5, 10.0)
MESH = pl.DeviceIdType.MESH
AXES = ("slab", "py", "pz")
UNROLLED = 64
PLAN = (2, 3)


def times(coeff, columns):
    total = {}
    for k, c in coeff.items():
        for q, value in columns[k].items():
            term = c * value
            total[q] = total[q] + term if q in total else term
    return total


def dot(left, right):
    total = None
    for q, value in left.items():
        if q in right:
            term = value * right[q]
            total = term if total is None else total + term
    return 0.0 if total is None else total


def advance(j, steps, inner, shifts, taus, removed, betas):
    vectors = [{k: 1.0} for k in range(j + 1)]
    image_of = [{**removed[k], k + 1: betas[k]} for k in range(j)]
    for i in range(steps):
        column = {j + i + 1: 1.0, j + i: shifts[i]}
        if taus[i] is not None:
            column[j + i - 1] = taus[i]
        image_of.append(column)
    gram, lowered = {}, []
    for n in range(j, j + steps):
        for k in range(len(lowered), n + 1):
            lowered.append({
                q: dot(vectors[k], {b: inner[q, b] for b in vectors[k]})
                for q in range(n + 1)})
            for l in range(k + 1):
                gram[k, l] = gram[l, k] = dot(vectors[l], lowered[k])
        known = {n: shifts[n - j]}
        if n > j:
            known[n - 1] = betas[n - 1]
            rest = times(vectors[n], image_of)
            for k, y in known.items():
                for q, value in vectors[k].items():
                    rest[q] = rest[q] - y * value if q in rest else -y * value
        else:
            if taus[0] is not None:
                known[n - 1] = taus[0]
            rest = {n + 1: 1.0}
        rest_lowered = {
            q: dot(rest, {b: inner[q, b] for b in rest}) for q in range(n + 2)}
        along = {k: dot(vectors[k], rest_lowered) for k in range(n + 1)}
        first = {
            k: along[k] + dot(known, {l: gram[k, l] for l in known}) for k in range(n + 1)}
        excess = {k: first[k] - known[k] if k in known else first[k] for k in range(n + 1)}
        coeffs = {
            k: along[k] - dot(excess, {
                l: gram[k, l] - 1.0 if k == l else gram[k, l] for l in range(n + 1)})
            for k in range(n + 1)}
        square = dot(rest, rest_lowered)
        for k in range(n + 1):
            back = dot(coeffs, {l: gram[k, l] for l in range(n + 1)})
            square = square + coeffs[k] * (back - 2.0 * along[k])
        beta = jnp.sqrt(jnp.maximum(square, 0.0) + EPSILON)
        inverse = 1.0 / beta
        image = dict(rest)
        for k in range(n + 1):
            for q, value in vectors[k].items():
                term = coeffs[k] * value
                image[q] = image[q] - term if q in image else -term
        vectors.append({q: value * inverse for q, value in image.items()})
        removed.append({k: coeffs[k] + known[k] if k in known else coeffs[k] for k in coeffs})
        betas.append(beta)
    return vectors[j + 1:]


def basis_of(j, steps, removed, betas, start):
    if j == 0:
        return [start + shift for shift in FIRST_SHIFTS[:steps]], [None] * steps
    shift, beta = removed[j - 1][j - 1], betas[j - 1]
    return [shift] * steps, [beta] + [beta * beta] * (steps - 1)


def kernel(sizes, per_cell, x_hbm, pot_hbm, out_ref, tri_ref, x_ref, pot_ref, work, ysend, zface, yface, xface,
           rz, ry, rx, slots, send_sem, recv_sem, stat_send, stat_recv, load_sem):
    Z, Y, X = x_hbm.shape
    S, A, B = sizes
    n = S * A * B
    slab, py, pz = (lax.axis_index(name) for name in AXES)
    me = (slab * A + py) * B + pz
    partner = lax.rem(slab + 1, S)

    def to_others(act):
        if n <= UNROLLED:
            slabs = [lax.rem(slab + i, S) for i in range(S)]
            pys = [lax.rem(py + i, A) for i in range(A)]
            pzs = [lax.rem(pz + i, B) for i in range(B)]
            far = sorted(
                ((i, j, k) for i in range(S) for j in range(A) for k in range(B)),
                key=lambda t: -(min(t[1], A - t[1]) + min(t[2], B - t[2])),
            )
            for i, j, k in far:
                if i or j or k:
                    act((slabs[i], pys[j], pzs[k]))
        else:
            def step(d, carry):
                t = lax.rem(me + d, n)
                act((t // (A * B), lax.rem(t // B, A), lax.rem(t, B)))
                return carry
            lax.fori_loop(1, n, step, 0)

    def halo_copies(p, zlo, zhi, block):
        def copy(src, dst, side, target):
            return pltpu.make_async_remote_copy(
                src_ref=src, dst_ref=dst, send_sem=send_sem.at[p, side],
                recv_sem=recv_sem.at[p, side], device_id=target, device_id_type=MESH)
        return (
            (pz < B - 1, pz > 0, copy(zhi, rz.at[p, 0], 0, (slab, py, pz + 1))),
            (pz > 0, pz < B - 1, copy(zlo, rz.at[p, 1], 1, (slab, py, pz - 1))),
            (py < A - 1, py > 0, copy(ysend.at[p, 1], ry.at[p, 0], 2, (slab, py + 1, pz))),
            (py > 0, py < A - 1, copy(ysend.at[p, 0], ry.at[p, 1], 3, (slab, py - 1, pz))),
            (None, None, copy(block, rx.at[p], 4, (partner, py, pz))),
        )

    def when(cond, act):
        if cond is None:
            act()
        else:
            pl.when(cond)(act)

    def exchange(p, zlo, zhi, block):
        copies = halo_copies(p, zlo, zhi, block)
        for sends, _, copy in copies:
            when(sends, copy.start)
        return copies

    def arrived(copies):
        for _, receives, copy in copies:
            when(receives, copy.wait_recv)

    def sent(copies):
        for sends, _, copy in copies:
            when(sends, copy.wait_send)

    def stat_copy(p, target):
        return pltpu.make_async_remote_copy(
            src_ref=slots.at[p, me], dst_ref=slots.at[p, me], send_sem=stat_send.at[p],
            recv_sem=stat_recv.at[p], device_id=target, device_id_type=MESH)

    def wait_all(p, sem):
        span = slots.at[p, pl.ds(0, n - 1)]
        pltpu.make_async_copy(span, span, sem).wait()

    lane = lax.broadcasted_iota(jnp.int32, (Y, X), 1)
    row = lax.broadcasted_iota(jnp.int32, (Y, X), 0)
    has_low = (slab > 0).astype(jnp.float32)
    has_high = (slab < S - 1).astype(jnp.float32)

    def stencil(z, own, zf, yf, xf):
        here = own(z)
        below = own(z - 1) if z > 0 else zf(0)
        above = own(z + 1) if z < Z - 1 else zf(1)
        ylow = jnp.where(row == 0, yf(0, z), pltpu.roll(here, 1, 0))
        yhigh = jnp.where(row == Y - 1, yf(1, z), pltpu.roll(here, Y - 1, 0))
        side = xf(z)
        xlow = pltpu.roll(jnp.where(lane == X - 1, side * has_low, here), 1, 1)
        xhigh = pltpu.roll(jnp.where(lane == 0, side * has_high, here), X - 1, 1)
        return (above + below) + (yhigh + ylow) + (xhigh + xlow)

    def fold(value):
        return jnp.sum(value.reshape(Y // 8, 8, X), axis=0)

    def share(p, sums):
        rows = [jnp.sum(v, axis=0, keepdims=True) for v in sums]
        height = -(-len(rows) // 8) * 8
        rows = rows + [jnp.zeros((1, X), jnp.float32)] * (height - len(rows))
        totals = jnp.sum(jnp.concatenate(rows, axis=0), axis=1, keepdims=True)
        at = lax.broadcasted_iota(jnp.int32, (height, X), 0)
        lanes = lax.broadcasted_iota(jnp.int32, (height, X), 1)
        slots[p, me] = jnp.sum(jnp.where(at == lanes, totals, 0.0), axis=0, keepdims=True)
        to_others(lambda target: stat_copy(p, target).start())

    def gathered(p, count):
        wait_all(p, stat_recv.at[p])
        total = jnp.sum(slots[p], axis=0) * per_cell
        return [jnp.broadcast_to(total[:, s:s + 1], (1, X)) for s in range(count)]

    barrier = pltpu.get_barrier_semaphore()
    to_others(lambda t: pl.semaphore_signal(barrier, inc=1, device_id=t, device_id_type=MESH))
    loads = (pltpu.make_async_copy(x_hbm, x_ref, load_sem.at[0]),
             pltpu.make_async_copy(pot_hbm, pot_ref, load_sem.at[1]))
    for load in loads:
        load.start()
    for p in range(ITERS):
        for side, missing in ((0, pz == 0), (1, pz == B - 1)):
            @pl.when(missing)
            def _(p=p, side=side):
                rz[p, side] = jnp.zeros((Y, X), jnp.float32)
        for side, missing in ((0, py == 0), (1, py == A - 1)):
            @pl.when(missing)
            def _(p=p, side=side):
                ry[p, side] = jnp.zeros((Z, X), jnp.float32)
    for load in loads:
        load.wait()
    for z in range(Z):
        ysend[0, 0, z:z + 1] = x_ref[z, 0:1, :]
        ysend[0, 1, z:z + 1] = x_ref[z, Y - 1:Y, :]
    pl.semaphore_wait(barrier, n - 1)

    pending = [exchange(0, x_ref.at[0], x_ref.at[Z - 1], x_ref)]

    def vector(k):
        if k == 0 and base == 0:
            return (lambda z: x_ref[z]), *faces(0)
        return ((lambda z: out_ref[k, z]), (lambda f: zface[k, f]),
                (lambda f, z: yface[k, f, z:z + 1, :]), (lambda z: xface[k, z]),
                (lambda f: yface[k, f]))

    def faces(e):
        return ((lambda f: rz[e, f]), (lambda f, z: ry[e, f, z:z + 1, :]), (lambda z: rx[e, z]),
                (lambda f: ry[e, f]))

    def powered(e):
        return (lambda z: work[e - 1, z]), *faces(e)

    removed, betas, inner, fresh = [], [], {}, range(1)
    start = jnp.zeros((1, X), jnp.float32)
    base, applied = 0, 0
    for phase, steps in enumerate(PLAN):
        last = base + steps == ITERS
        shifts, taus = basis_of(base, steps, removed, betas, start)
        held = [vector(k) for k in range(base + 1)]
        pairs, sums = [], []

        def measure(n, held=held, pairs=pairs, sums=sums):
            totals = [jnp.zeros((8, X), jnp.float32)] * (n + 1)
            for z in range(Z):
                newest = held[n][0](z)
                for k in range(n + 1):
                    totals[k] = totals[k] + fold(held[k][0](z) * newest)
            pairs.extend((k, n) for k in range(n + 1))
            sums.extend(totals)

        if phase == 0:
            for v in fresh:
                measure(v)
            arrived(pending[0])
        for i in range(steps):
            own, zf, yf, xf, _ = held[base + i]
            applied += 1
            ends = applied == ITERS
            for z in range(Z):
                image = (((DIAGONAL - shifts[i]) + pot_ref[z]) * own(z)
                         - stencil(z, own, zf, yf, xf))
                if taus[i] is not None:
                    image = image - taus[i] * held[base + i - 1][0](z)
                work[applied - 1, z] = image
                if not ends:
                    ysend[applied, 0, z:z + 1] = image[0:1]
                    ysend[applied, 1, z:z + 1] = image[Y - 1:Y]
            held.append(powered(applied))
            if not ends:
                pending.append(exchange(applied, work.at[applied - 1, 0],
                                        work.at[applied - 1, Z - 1], work.at[applied - 1]))
            if i == 0 and phase > 0:
                for v in fresh:
                    measure(v)
            measure(base + i + 1)
            if i < steps - 1:
                arrived(pending[applied])
        share(phase, sums)
        stats = gathered(phase, len(sums))
        if phase == 0:
            scale = 1.0 / jnp.sqrt(stats[0] + EPSILON)
            stats = [s * scale * scale for s in stats]
        for (k, l), value in zip(pairs, stats):
            inner[k, l] = inner[l, k] = value
        found = advance(base, steps, inner, shifts, taus, removed, betas)
        for v in range(base, base + steps):
            tri_ref[0:1, v:v + 1] = removed[v][v][:, 0:1]
            tri_ref[1:2, v:v + 1] = betas[v][:, 0:1]
        if phase == 0:
            found = [{q: t * scale for q, t in coords.items()} for coords in found]
        if not last:
            arrived(pending[applied])

        def fill(get, put, only_last):
            columns = [get(held[q]) for q in range(base + steps + 1)]
            if phase == 0 and not (only_last and len(PLAN) == 2):
                put(0, columns[0] * scale)
            for i, coords in enumerate(found):
                if only_last and phase == len(PLAN) - 2 and i < steps - 1:
                    continue
                total = None
                for q in sorted(coords, reverse=True):
                    term = coords[q] * columns[q]
                    total = term if total is None else total + term
                put(base + 1 + i, total)

        def putter(ref, *index):
            def put(k, value):
                ref[(k,) + index] = value
            return put

        for z in range(Z):
            fill(lambda h: h[0](z), putter(out_ref, z), False)
            if not last:
                fill(lambda h: h[3](z), putter(xface, z), True)
        if not last:
            for f in range(2):
                fill(lambda h: h[1](f), putter(zface, f), True)
                fill(lambda h: h[4](f), putter(yface, f), True)
        inner = {pair: value for pair, value in inner.items() if max(pair) <= base}
        fresh = range(base + 1, base + steps + 1)
        base += steps

    for copies in pending:
        sent(copies)
    for p in range(len(PLAN)):
        wait_all(p, stat_send.at[p])


def write_out(basis_ref, tri_ref, basis_out, tri_out, sems):
    copies = (pltpu.make_async_copy(basis_ref, basis_out, sems.at[0]),
              pltpu.make_async_copy(tri_ref, tri_out, sems.at[1]))
    for copy in copies:
        copy.start()
    for copy in copies:
        copy.wait()


def shards(sizes, start_vector, potential):
    Z, Y, X = start_vector.shape
    n = sizes[0] * sizes[1] * sizes[2]
    f32 = jnp.float32
    vmem = pl.BlockSpec(memory_space=pltpu.VMEM)
    hbm = pl.BlockSpec(memory_space=pl.ANY)
    basis, tri = pl.pallas_call(
        functools.partial(kernel, sizes, 1.0 / (start_vector.size * n)),
        out_shape=(pltpu.VMEM((ITERS + 1, Z, Y, X), f32), pltpu.VMEM((2, ITERS), f32)),
        in_specs=[hbm, hbm],
        out_specs=(vmem, vmem),
        scratch_shapes=[
            pltpu.VMEM((Z, Y, X), f32),
            pltpu.VMEM((Z, Y, X), f32),
            pltpu.VMEM((ITERS, Z, Y, X), f32),
            pltpu.VMEM((ITERS, 2, Z, X), f32),
            pltpu.VMEM((ITERS, 2, Y, X), f32),
            pltpu.VMEM((ITERS, 2, Z, X), f32),
            pltpu.VMEM((ITERS, Z, Y, X), f32),
            pltpu.VMEM((ITERS, 2, Y, X), f32),
            pltpu.VMEM((ITERS, 2, Z, X), f32),
            pltpu.VMEM((ITERS, Z, Y, X), f32),
            pltpu.VMEM((ITERS, n, 1, X), f32),
            pltpu.SemaphoreType.DMA((ITERS, 5)),
            pltpu.SemaphoreType.DMA((ITERS, 5)),
            pltpu.SemaphoreType.DMA((ITERS,)),
            pltpu.SemaphoreType.DMA((ITERS,)),
            pltpu.SemaphoreType.DMA((2,)),
        ],
        compiler_params=pltpu.CompilerParams(collective_id=0, has_side_effects=True),
    )(start_vector, potential)
    return tuple(pl.pallas_call(
        write_out,
        out_shape=(jax.ShapeDtypeStruct(basis.shape, f32), jax.ShapeDtypeStruct(tri.shape, f32)),
        in_specs=[vmem, vmem],
        out_specs=(hbm, hbm),
        scratch_shapes=[pltpu.SemaphoreType.DMA((2,))],
    )(pltpu.with_memory_space_constraint(basis, pltpu.VMEM), pltpu.with_memory_space_constraint(tri, pltpu.VMEM)))


def solution(mesh):
    sizes = tuple(mesh.shape[name] for name in AXES)
    in_specs = (P("pz", "py", "slab"), P("pz", "py", "slab"))
    out_specs = (P(None, "pz", "py", "slab"), P())
    return jax.shard_map(functools.partial(shards, sizes), mesh=mesh, in_specs=in_specs,
                         out_specs=out_specs, check_vma=False)
```

profile of v0, /device:TPU:0, one launch (start us, length us, event | category | flops | bytes accessed | tf_op | source)
XLA Modules:
  0.0 31.8 jit_solution(11531657107276146349)
XLA Ops:
  0.6 30.2 %shard_map.41 = (f32[6,8,32,128]{3,2,1,0:T(8,128)S(1)}, f32[2,5]{1,0:T(2,128)S(1)}) custom-call(f32[8,32,128]{2,1,0:T(8,128)} %x_hbm.1, f32[8,32,128]{2,1,0:T(8,128)} %pot_hbm.1), custom_call_target="tpu_custom_call" | custom-call | tf_op jit(solution)/shard_map/pallas_call | solution.py:353
  30.9 0.9 %shard_map.42 = (f32[6,8,32,128]{3,2,1,0:T(8,128)}, f32[2,5]{1,0:T(2,128)}) custom-call(f32[6,8,32,128]{3,2,1,0:T(8,128)S(1)} %get-tuple-element.4.basis_ref, f32[2,5]{1,0:T(2,128)S(1)} %get-tuple-element.5.tri_ref), custom_call_target="tpu_custom_call" | custom-call | tf_op jit(solution)/shard_map/pallas_call | solution.py:378
where the time goes:
time: 31.9 us; the launch traced here: 31.8 us
  Pallas kernels  31.1 us (97%)
  between operations  0.64 us (2%)
    pallas_call x1, Pallas kernels, shards(): pl.pallas_call(functools.partial(kernel, sizes, 1.0 / (start_vector.size...  30.2 us
    pallas_call x1, Pallas kernels, shards(): pl.pallas_call(write_out, out_shape=(jax.ShapeDtypeStruct(basis.shape, f3...  0.9 us

commit v1 on v0

v1 whole, which is shorter than its diff:
```python
import functools

import jax
import jax.numpy as jnp
from jax import lax
from jax.experimental import pallas as pl
from jax.experimental.pallas import tpu as pltpu
from jax.sharding import PartitionSpec as P

ITERS = 5
EPSILON = 1e-06
DIAGONAL = 6.0
SUBLANES = 8
MESH = pl.DeviceIdType.MESH
AXES = ("slab", "py", "pz")
UNROLLED = 64
CENTER = 8.25
LEAST_SQUARE, MOST_SQUARE = 0.25, 40.0
LEAST_SHIFT, MOST_SHIFT = 0.5, 16.5
VECTOR, POTENTIAL = 0, 1


def times(coeff, columns):
    total = {}
    for k, c in coeff.items():
        for q, value in columns[k].items():
            term = c * value
            total[q] = total[q] + term if q in total else term
    return total


def dot(left, right):
    total = None
    for q, value in left.items():
        if q in right:
            term = value * right[q]
            total = term if total is None else total + term
    return 0.0 if total is None else total


def advance(steps, inner, shifts, taus, removed, betas):
    vectors = [{0: 1.0}]
    image_of = []
    for i in range(steps):
        column = {i + 1: 1.0, i: shifts[i]}
        if taus[i] is not None:
            column[i - 1] = taus[i]
        image_of.append(column)
    gram, lowered = {}, []
    for n in range(steps):
        for k in range(len(lowered), n + 1):
            lowered.append({
                q: dot(vectors[k], {b: inner[q, b] for b in vectors[k]})
                for q in range(n + 1)})
            for l in range(k + 1):
                gram[k, l] = gram[l, k] = dot(vectors[l], lowered[k])
        known = {n: shifts[n]}
        if n > 0:
            known[n - 1] = betas[n - 1]
            rest = times(vectors[n], image_of)
            for k, y in known.items():
                for q, value in vectors[k].items():
                    rest[q] = rest[q] - y * value if q in rest else -y * value
        else:
            rest = {n + 1: 1.0}
        rest_lowered = {
            q: dot(rest, {b: inner[q, b] for b in rest}) for q in range(n + 2)}
        along = {k: dot(vectors[k], rest_lowered) for k in range(n + 1)}
        first = {
            k: along[k] + dot(known, {l: gram[k, l] for l in known}) for k in range(n + 1)}
        excess = {k: first[k] - known[k] if k in known else first[k] for k in range(n + 1)}
        coeffs = {
            k: along[k] - dot(excess, {
                l: gram[k, l] - 1.0 if k == l else gram[k, l] for l in range(n + 1)})
            for k in range(n + 1)}
        square = dot(rest, rest_lowered)
        for k in range(n + 1):
            back = dot(coeffs, {l: gram[k, l] for l in range(n + 1)})
            square = square + coeffs[k] * (back - 2.0 * along[k])
        beta = jnp.sqrt(jnp.maximum(square, 0.0) + EPSILON)
        inverse = 1.0 / beta
        image = dict(rest)
        for k in range(n + 1):
            for q, value in vectors[k].items():
                term = coeffs[k] * value
                image[q] = image[q] - term if q in image else -term
        vectors.append({q: value * inverse for q, value in image.items()})
        removed.append({k: coeffs[k] + known[k] if k in known else coeffs[k] for k in coeffs})
        betas.append(beta)
    return vectors[1:]


def kernel(sizes, per_cell, x_hbm, pot_hbm, out_ref, tri_ref, cells, ext, swapped, slots,
           send_sem, recv_sem, side_send, side_recv, near_send, near_recv, swap_send, swap_recv,
           stat_send, stat_recv, load_sem):
    Z, Y, X = x_hbm.shape
    S, A, B = sizes
    n = S * A * B
    H = Z // 2
    D = ITERS
    T = SUBLANES
    ZE, YE = H + 2 * D, Y + 2 * T
    slab, py, pz = (lax.axis_index(name) for name in AXES)
    me = (slab * A + py) * B + pz
    partner = (1 - slab, py, pz)
    first_plane = D - slab * H
    inside = pl.ds(T, Y)

    def to_others(act):
        if n <= UNROLLED:
            slabs = [lax.rem(slab + i, S) for i in range(S)]
            pys = [lax.rem(py + i, A) for i in range(A)]
            pzs = [lax.rem(pz + i, B) for i in range(B)]
            far = sorted(
                ((i, j, k) for i in range(S) for j in range(A) for k in range(B)),
                key=lambda t: -(min(t[1], A - t[1]) + min(t[2], B - t[2])),
            )
            for i, j, k in far:
                if i or j or k:
                    act((slabs[i], pys[j], pzs[k]))
        else:
            def step(d, carry):
                t = lax.rem(me + d, n)
                act((t // (A * B), lax.rem(t // B, A), lax.rem(t, B)))
                return carry
            lax.fori_loop(1, n, step, 0)

    def source(array):
        return cells.at[0] if array == VECTOR else ext

    def remote(src, dst, sent, received, target):
        return pltpu.make_async_remote_copy(
            src_ref=src, dst_ref=dst, send_sem=sent, recv_sem=received,
            device_id=target, device_id_type=MESH)

    def reach(array):
        return D if array == VECTOR else D - 1

    def within(step, position, size):
        if step == 0:
            return None
        return position + step >= 0 if step < 0 else position + step < size

    def guarded(conditions, act):
        conditions = [c for c in conditions if c is not None]
        if not conditions:
            act()
        else:
            pl.when(functools.reduce(jnp.logical_and, conditions))(act)

    def plane_of(t, side, d):
        z = t * H - d if side == 0 else t * H + H - 1 + d
        return z // Z, z % Z

    def lands(side, d):
        return D - d if side == 0 else D + H - 1 + d

    def rows(step, count, sending):
        if step == 0:
            return inside
        if step < 0:
            return pl.ds(T + Y - count, count) if sending else pl.ds(T - count, count)
        return pl.ds(T, count) if sending else pl.ds(T + Y, count)

    def index(array, side, d, step):
        return ((array * 2 + side) * D + d - 1) * 3 + step + 1

    def plane_copy(array, t, side, d, step, core):
        q, z = plane_of(t, side, d)
        count = reach(array) - d
        ref = source(array)
        i = index(array, side, d, step)
        return remote(
            ref.at[core, z + first_plane, rows(step, count, True)],
            ref.at[core, lands(side, d), rows(step, count, False)],
            send_sem.at[i, t], recv_sem.at[i, core], (t, py - step, pz - q))

    def planes(w, sending, act):
        for t in range(2):
            for side in range(2):
                wanted = [(array, d) for array, d in ((VECTOR, w), (POTENTIAL, w - 1))
                          if 1 <= d <= reach(array) and plane_of(t, side, d)[0] != 0]
                for q in sorted({plane_of(t, side, d)[0] for _, d in wanted}, key=abs):
                    mine = [(a, d) for a, d in wanted if plane_of(t, side, d)[0] == q]
                    sign = -1 if sending else 1
                    own = None if sending else slab == t

                    def straight(t=t, side=side, mine=mine):
                        for array, d in mine:
                            act(array, t, side, d, 0)

                    guarded([own, within(sign * q, pz, B)], straight)
                    for step in (-1, 1):
                        beside = [(a, d) for a, d in mine if reach(a) > d]
                        if beside:
                            def corner(t=t, side=side, beside=beside, step=step):
                                for array, d in beside:
                                    act(array, t, side, d, step)

                            guarded([own, within(sign * q, pz, B), within(sign * step, py, A)], corner)

    def start_plane(*key):
        plane_copy(*key, slab).start()

    def finish_plane(*key):
        plane_copy(*key, slab).wait_send()

    def take_plane(*key):
        for core in range(2):
            plane_copy(*key, core).wait_recv()

    def side_copy(array, t, step, core):
        ref = source(array)
        count = reach(array)
        return remote(
            ref.at[core, pl.ds(first_plane, Z), rows(step, count, True)],
            ref.at[core, pl.ds(D - t * H, Z), rows(step, count, False)],
            side_send.at[array, step > 0 and 1 or 0, t], side_recv.at[array, step > 0 and 1 or 0, core],
            (t, py - step, pz))

    def sides(sending, act):
        for step in (-1, 1):
            def both(step=step):
                for array in (VECTOR, POTENTIAL):
                    for other in range(2):
                        act(array, other, step)
            guarded([within(-step if sending else step, py, A)], both)

    def near_copy(array):
        ref = source(array)
        return remote(
            ref.at[slab, pl.ds(first_plane, Z), inside],
            ref.at[slab, pl.ds(D - (1 - slab) * H, Z), inside],
            near_send.at[array], near_recv.at[array], partner)

    def near_arrival(array):
        ref = source(array)
        span = ref.at[1 - slab, pl.ds(first_plane, Z), inside]
        return remote(span, span, near_send.at[array], near_recv.at[array], partner)

    def side_arrival(array, core, step):
        ref = source(array)
        span = ref.at[core, pl.ds(first_plane, Z), rows(step, reach(array), False)]
        k = step > 0 and 1 or 0
        return remote(span, span, side_send.at[array, k, 0], side_recv.at[array, k, core], partner)

    def swap_copy(level):
        return remote(
            cells.at[level, 1 - slab, pl.ds(D, H), inside], swapped.at[level - 1],
            swap_send.at[level - 1], swap_recv.at[level - 1], partner)

    def stat_copy(p, target):
        return remote(slots.at[p, me], slots.at[p, me], stat_send.at[p], stat_recv.at[p], target)

    def wait_all(p, sem):
        span = slots.at[p, pl.ds(0, n - 1)]
        pltpu.make_async_copy(span, span, sem).wait()

    def fold(value):
        return jnp.sum(value.reshape(value.shape[0] // T, T, X), axis=0)

    def share(p, sums):
        lines = [jnp.sum(v, axis=0, keepdims=True) for v in sums]
        height = -(-len(lines) // T) * T
        lines = lines + [jnp.zeros((1, X), jnp.float32)] * (height - len(lines))
        totals = jnp.sum(jnp.concatenate(lines, axis=0), axis=1, keepdims=True)
        at = lax.broadcasted_iota(jnp.int32, (height, X), 0)
        lanes = lax.broadcasted_iota(jnp.int32, (height, X), 1)
        slots[p, me] = jnp.sum(jnp.where(at == lanes, totals, 0.0), axis=0, keepdims=True)

    def gathered(p, count):
        wait_all(p, stat_recv.at[p])
        total = jnp.sum(slots[p], axis=0) * per_cell
        return [jnp.broadcast_to(total[:, s:s + 1], (1, X)) for s in range(count)]

    barrier = pltpu.get_barrier_semaphore()
    to_others(lambda t: pl.semaphore_signal(barrier, inc=1, device_id=t, device_id_type=MESH))
    loads = [pltpu.make_async_copy(
        hbm, source(array).at[slab, pl.ds(first_plane, Z), inside], load_sem.at[array])
        for array, hbm in ((VECTOR, x_hbm), (POTENTIAL, pot_hbm))]
    for load in loads:
        load.start()

    plane = pz * Z + slab * H - D
    present = [jnp.logical_and(plane + e >= 0, plane + e < B * Z) for e in range(ZE)]
    for e in range(ZE):
        if D <= e < D + H:
            continue
        @pl.when(jnp.logical_not(present[e]))
        def _(e=e):
            for ref in (cells.at[0], ext):
                for core in range(2):
                    ref[core, e] = jnp.zeros((YE, X), jnp.float32)
    for missing, at in ((py == 0, 0), (py == A - 1, T + Y)):
        @pl.when(missing)
        def _(at=at):
            for ref in (cells.at[0], ext):
                for core in range(2):
                    for e in range(ZE):
                        ref[core, e, at:at + T] = jnp.zeros((T, X), jnp.float32)
    for load in loads:
        load.wait()

    def rough():
        lane = lax.broadcasted_iota(jnp.int32, (Y, X), 1)
        row = lax.broadcasted_iota(jnp.int32, (Y, X), 0)

        def apply(own, z):
            here = own(z)
            total = (jnp.where(row == 0, 0.0, pltpu.roll(here, 1, 0))
                     + jnp.where(row == Y - 1, 0.0, pltpu.roll(here, Y - 1, 0))
                     + jnp.where(lane == 0, 0.0, pltpu.roll(here, 1, 1))
                     + jnp.where(lane == X - 1, 0.0, pltpu.roll(here, X - 1, 1)))
            for beside in (z - 1, z + 1):
                if 0 <= beside < Z:
                    total = total + own(beside)
            return ext[slab, first_plane + z, inside] * here - total

        start = lambda z: cells[0, slab, first_plane + z, inside]
        once = lambda z: out_ref[0, z]
        sums = [jnp.zeros((T, X), jnp.float32)] * 5
        for z in range(Z):
            out_ref[0, z] = apply(start, z)
        for z in range(Z):
            zero, one, two = start(z), once(z), apply(once, z)
            for i, (u, v) in enumerate(((zero, zero), (zero, one), (one, one), (one, two), (two, two))):
                sums[i] = sums[i] + fold(u * v)
        return sums

    share(0, rough())
    pl.semaphore_wait(barrier, n - 1)

    to_others(lambda target: stat_copy(0, target).start())
    for array in (VECTOR, POTENTIAL):
        near_copy(array).start()
    planes(1, True, start_plane)
    sides(True, lambda array, t, step: side_copy(array, t, step, slab).start())
    for w in range(2, D + 1):
        planes(w, True, start_plane)

    m0, m1, m2, m3, m4 = gathered(0, 5)
    some = m0 > 1e-30
    over = 1.0 / jnp.where(some, m0, 1.0)
    m1, m2, m3, m4 = m1 * over, m2 * over, m3 * over, m4 * over
    c2 = m2 - m1 * m1
    c3 = m3 - 3.0 * m1 * m2 + 2.0 * m1 * m1 * m1
    c4 = m4 - 4.0 * m1 * m3 + 6.0 * m1 * m1 * m2 - 3.0 * m1 * m1 * m1 * m1
    down = 1.0 / jnp.maximum(c2, 1e-3)
    slope = c3 * down
    bound = lambda value, low, high: jnp.minimum(jnp.maximum(value, low), high)
    alpha = [bound(jnp.where(some, DIAGONAL + a, CENTER), LEAST_SHIFT, MOST_SHIFT) for a in (m1, m1 + slope)]
    square = [bound(b, LEAST_SQUARE, MOST_SQUARE) for b in (c2, c4 * down - c2 - slope * slope)]
    shifts = [alpha[0]] + [alpha[1]] * (D - 1)
    taus = [None, square[0]] + [square[1]] * (D - 2)

    lane = lax.broadcasted_iota(jnp.int32, (YE, X), 1)
    low_rows, high_rows = (py > 0).astype(jnp.float32), (py < A - 1).astype(jnp.float32)

    def level(l, e):
        left, right = cells[l - 1, 0, e], cells[l - 1, 1, e]
        up = [pltpu.roll(v, 1, 1) for v in (left, right)]
        down = [pltpu.roll(v, X - 1, 1) for v in (left, right)]
        along = (jnp.where(lane == 0, 0.0, up[0]) + jnp.where(lane == X - 1, down[1], down[0]),
                 jnp.where(lane == 0, up[0], up[1]) + jnp.where(lane == X - 1, 0.0, down[1]))
        for core, here in enumerate((left, right)):
            around = (cells[l - 1, core, e - 1] + cells[l - 1, core, e + 1]
                      + (pltpu.roll(here, 1, 0) + pltpu.roll(here, YE - 1, 0)) + along[core])
            image = ((DIAGONAL - shifts[l - 1]) + ext[core, e]) * here - around
            if taus[l - 1] is not None:
                image = image - taus[l - 1] * cells[l - 2, core, e]
            if not D <= e < D + H:
                image = image * present[e].astype(jnp.float32)
            cells[l, core, e, inside] = image[T:T + Y]
            if l < D:
                cells[l, core, e, 0:T] = image[0:T] * low_rows
                cells[l, core, e, T + Y:YE] = image[T + Y:YE] * high_rows

    def measure(pairs):
        sums = [jnp.zeros((T, X), jnp.float32)] * len(pairs)
        for core in range(2):
            for e in range(D, D + H):
                held = {k: cells[k, core, e, inside] for k in sorted({k for pair in pairs for k in pair})}
                for i, (k, l) in enumerate(pairs):
                    sums[i] = sums[i] + fold(held[k] * held[l])
        return sums

    for array in (VECTOR, POTENTIAL):
        near_arrival(array).wait_recv()
    sides(False, lambda array, core, step: side_arrival(array, core, step).wait_recv())
    early = [(k, l) for l in range(D) for k in range(l + 1)]
    late = [(k, D) for k in range(D + 1)]
    for w in range(D + 1):
        if w:
            planes(w, False, take_plane)
        for l in range(1, D + 1):
            for e in range(l, ZE - l):
                if l + max(D - e, e - (D + H - 1)) == w:
                    level(l, e)
        if 1 <= w:
            swap_copy(w).start()
        if w == D - 1:
            sums = measure(early)
    sums = sums + measure(late)
    share(1, sums)
    to_others(lambda target: stat_copy(1, target).start())
    stats = gathered(1, len(sums))
    scale = 1.0 / jnp.sqrt(stats[0] + EPSILON)
    inner = {}
    for (k, l), value in zip(early + late, stats):
        inner[k, l] = inner[l, k] = value * scale * scale
    removed, betas = [], []
    found = advance(D, inner, shifts, taus, removed, betas)
    for v in range(D):
        tri_ref[0:1, v:v + 1] = removed[v][v][:, 0:1]
        tri_ref[1:2, v:v + 1] = betas[v][:, 0:1]
    found = [{q: t * scale for q, t in coords.items()} for coords in found]

    for l in range(1, D + 1):
        swap_copy(l).wait_recv()
    for half in range(2):
        for i in range(H):
            if half == 0:
                z = slab * H + i
                columns = [cells[q, slab, D + i, inside] for q in range(D + 1)]
            else:
                z = (1 - slab) * H + i
                columns = [cells[0, slab, first_plane + z, inside]] + [swapped[q, i] for q in range(D)]
            out_ref[0, z] = columns[0] * scale
            for k, coords in enumerate(found):
                total = None
                for q in sorted(coords, reverse=True):
                    term = coords[q] * columns[q]
                    total = term if total is None else total + term
                out_ref[k + 1, z] = total

    for array in (VECTOR, POTENTIAL):
        near_copy(array).wait_send()
    sides(True, lambda array, t, step: side_copy(array, t, step, slab).wait_send())
    for w in range(1, D + 1):
        planes(w, True, finish_plane)
    for l in range(1, D + 1):
        swap_copy(l).wait_send()
    for p in range(2):
        wait_all(p, stat_send.at[p])


def write_out(basis_ref, tri_ref, basis_out, tri_out, sems):
    copies = (pltpu.make_async_copy(basis_ref, basis_out, sems.at[0]),
              pltpu.make_async_copy(tri_ref, tri_out, sems.at[1]))
    for copy in copies:
        copy.start()
    for copy in copies:
        copy.wait()


def shards(sizes, start_vector, potential):
    Z, Y, X = start_vector.shape
    n = sizes[0] * sizes[1] * sizes[2]
    f32 = jnp.float32
    H, D, T = Z // 2, ITERS, SUBLANES
    assert sizes[0] == 2 and Z % 2 == 0 and H <= D and Y >= D and Y % T == 0
    vmem = pl.BlockSpec(memory_space=pltpu.VMEM)
    hbm = pl.BlockSpec(memory_space=pl.ANY)
    dma = pltpu.SemaphoreType.DMA
    extended = (2, H + 2 * D, Y + 2 * T, X)
    basis, tri = pl.pallas_call(
        functools.partial(kernel, sizes, 1.0 / (start_vector.size * n)),
        out_shape=(pltpu.VMEM((D + 1, Z, Y, X), f32), pltpu.VMEM((2, D), f32)),
        in_specs=[hbm, hbm],
        out_specs=(vmem, vmem),
        scratch_shapes=[
            pltpu.VMEM((D + 1,) + extended, f32),
            pltpu.VMEM(extended, f32),
            pltpu.VMEM((D, H, Y, X), f32),
            pltpu.VMEM((2, n, 1, X), f32),
            dma((2 * 2 * D * 3, 2)),
            dma((2 * 2 * D * 3, 2)),
            dma((2, 2, 2)),
            dma((2, 2, 2)),
            dma((2,)),
            dma((2,)),
            dma((D,)),
            dma((D,)),
            dma((2,)),
            dma((2,)),
            dma((2,)),
        ],
        compiler_params=pltpu.CompilerParams(collective_id=0, has_side_effects=True),
    )(start_vector, potential)
    return tuple(pl.pallas_call(
        write_out,
        out_shape=(jax.ShapeDtypeStruct(basis.shape, f32), jax.ShapeDtypeStruct(tri.shape, f32)),
        in_specs=[vmem, vmem],
        out_specs=(hbm, hbm),
        scratch_shapes=[dma((2,))],
    )(pltpu.with_memory_space_constraint(basis, pltpu.VMEM), pltpu.with_memory_space_constraint(tri, pltpu.VMEM)))


def solution(mesh):
    sizes = tuple(mesh.shape[name] for name in AXES)
    in_specs = (P("pz", "py", "slab"), P("pz", "py", "slab"))
    out_specs = (P(None, "pz", "py", "slab"), P())
    return jax.shard_map(functools.partial(shards, sizes), mesh=mesh, in_specs=in_specs,
                         out_specs=out_specs, check_vma=False)
```

time: 31.9 us -> 24.4 us (0.76)
  Pallas kernels: 31.1 us -> 23.6 us
    pallas_call x1, Pallas kernels: 30.2 us -> 22.7 us  [shards(): pl.pallas_call(functools.partial(kernel, sizes, 1.0 / (start_vector.size...]
where the time goes in v1:
time: 24.4 us; the launch traced here: 24.2 us
  Pallas kernels  23.6 us (97%)
  between operations  0.64 us (3%)
    pallas_call x1, Pallas kernels, shards(): pl.pallas_call(functools.partial(kernel, sizes, 1.0 / (start_vector.size...  22.7 us
    pallas_call x1, Pallas kernels, shards(): pl.pallas_call(write_out, out_shape=(jax.ShapeDtypeStruct(basis.shape, f3...  0.9 us

profile of v1, /device:TPU:0, one launch (start us, length us, event | category | flops | bytes accessed | tf_op | source)
XLA Modules:
  0.0 24.2 jit_solution(9548277822068869214)
XLA Ops:
  0.6 22.7 %shard_map.41 = (f32[6,8,32,128]{3,2,1,0:T(8,128)S(1)}, f32[2,5]{1,0:T(2,128)S(1)}) custom-call(f32[8,32,128]{2,1,0:T(8,128)} %x_hbm.1, f32[8,32,128]{2,1,0:T(8,128)} %pot_hbm.1), custom_call_target="tpu_custom_call" | custom-call | tf_op jit(solution)/shard_map/pallas_call | solution.py:466
  23.3 0.9 %shard_map.42 = (f32[6,8,32,128]{3,2,1,0:T(8,128)}, f32[2,5]{1,0:T(2,128)}) custom-call(f32[6,8,32,128]{3,2,1,0:T(8,128)S(1)} %get-tuple-element.4.basis_ref, f32[2,5]{1,0:T(2,128)S(1)} %get-tuple-element.5.tri_ref), custom_call_target="tpu_custom_call" | custom-call | tf_op jit(solution)/shard_map/pallas_call | solution.py:490

commit v2 on v1

--- a/solution.py
+++ b/solution.py
@@ -18,6 +18,7 @@
 LEAST_SQUARE, MOST_SQUARE = 0.25, 40.0
 LEAST_SHIFT, MOST_SHIFT = 0.5, 16.5
 VECTOR, POTENTIAL = 0, 1
+RELAY_RING, RELAY_WAVE = 4, 4
 
 
 def times(coeff, columns):
@@ -90,8 +91,8 @@
     return vectors[1:]
 
 
-def kernel(sizes, per_cell, x_hbm, pot_hbm, out_ref, tri_ref, cells, ext, swapped, slots,
-           send_sem, recv_sem, side_send, side_recv, near_send, near_recv, swap_send, swap_recv,
+def kernel(sizes, per_cell, x_hbm, pot_hbm, out_ref, tri_ref, cells, ext, swapped, relayed, slots,
+           send_sem, recv_sem, relay_send, relay_recv, onward_send, side_send, side_recv, near_send, near_recv, swap_send, swap_recv,
            stat_send, stat_recv, load_sem):
     Z, Y, X = x_hbm.shape
     S, A, B = sizes
@@ -175,6 +176,28 @@
             ref.at[core, lands(side, d), rows(step, count, False)],
             send_sem.at[i, t], recv_sem.at[i, core], (t, py - step, pz - q))
 
+    relays = [(a, d) for w in range(RELAY_WAVE, D + 1) for a, d in ((VECTOR, w), (POTENTIAL, w - 1))] if (
+        B == RELAY_RING and plane_of(0, 0, D)[0] == -1) else []
+
+    def relay_copy(k, t):
+        array, d = relays[k]
+        z = plane_of(t, t, d)[1]
+        return remote(source(array).at[slab, z + first_plane, inside], relayed.at[k],
+                      relay_send.at[k], relay_recv.at[k], (slab, py, B - 1 if t == 0 else 0))
+
+    def onward_copy(k, t):
+        array, d = relays[k]
+        return remote(relayed.at[k], source(array).at[slab, lands(t, d), inside], onward_send.at[k],
+                      recv_sem.at[index(array, t, d, 0), slab], (t, py, B - 2 if t == 0 else 1))
+
+    def each_relay(at, act):
+        for t in range(2):
+            if relays:
+                @pl.when(pz == at[t])
+                def _(t=t):
+                    for k in range(len(relays)):
+                        act(k, t)
+
     def planes(w, sending, act):
         for t in range(2):
             for side in range(2):
@@ -189,7 +212,10 @@
                         for array, d in mine:
                             act(array, t, side, d, 0)
 
-                    guarded([own, within(sign * q, pz, B)], straight)
+                    direct = None
+                    if sending and t == side and set(mine) & set(relays):
+                        direct = pz != 1 + t
+                    guarded([own, within(sign * q, pz, B), direct], straight)
                     for step in (-1, 1):
                         beside = [(a, d) for a, d in mine if reach(a) > d]
                         if beside:
@@ -331,12 +357,19 @@
     pl.semaphore_wait(barrier, n - 1)
 
     to_others(lambda target: stat_copy(0, target).start())
+    each_relay((1, 2), lambda k, t: relay_copy(k, t).start())
     for array in (VECTOR, POTENTIAL):
         near_copy(array).start()
     planes(1, True, start_plane)
     sides(True, lambda array, t, step: side_copy(array, t, step, slab).start())
     for w in range(2, D + 1):
         planes(w, True, start_plane)
+
+    def forward(k, t):
+        relay_copy(k, t).wait_recv()
+        onward_copy(k, t).start()
+
+    each_relay((B - 1, 0), forward)
 
     m0, m1, m2, m3, m4 = gathered(0, 5)
     some = m0 > 1e-30
@@ -436,6 +469,8 @@
     for array in (VECTOR, POTENTIAL):
         near_copy(array).wait_send()
     sides(True, lambda array, t, step: side_copy(array, t, step, slab).wait_send())
+    each_relay((1, 2), lambda k, t: relay_copy(k, t).wait_send())
+    each_relay((B - 1, 0), lambda k, t: onward_copy(k, t).wait_send())
     for w in range(1, D + 1):
         planes(w, True, finish_plane)
     for l in range(1, D + 1):
@@ -472,9 +507,13 @@
             pltpu.VMEM((D + 1,) + extended, f32),
             pltpu.VMEM(extended, f32),
             pltpu.VMEM((D, H, Y, X), f32),
+            pltpu.VMEM((2 * (D + 1 - RELAY_WAVE), Y, X), f32),
             pltpu.VMEM((2, n, 1, X), f32),
             dma((2 * 2 * D * 3, 2)),
             dma((2 * 2 * D * 3, 2)),
+            dma((2 * (D + 1 - RELAY_WAVE),)),
+            dma((2 * (D + 1 - RELAY_WAVE),)),
+            dma((2 * (D + 1 - RELAY_WAVE),)),
             dma((2, 2, 2)),
             dma((2, 2, 2)),
             dma((2,)),

time: 24.4 us -> 23.6 us (0.967)
  Pallas kernels: 23.6 us -> 22.8 us
    pallas_call x1, Pallas kernels: 22.7 us -> 21.9 us  [shards(): pl.pallas_call(functools.partial(kernel, sizes, 1.0 / (start_vector.size...]
where the time goes in v2:
time: 23.6 us; the launch traced here: 23.4 us
  Pallas kernels  22.8 us (97%)
  between operations  0.64 us (3%)
    pallas_call x1, Pallas kernels, shards(): pl.pallas_call(functools.partial(kernel, sizes, 1.0 / (start_vector.size...  21.9 us
    pallas_call x1, Pallas kernels, shards(): pl.pallas_call(write_out, out_shape=(jax.ShapeDtypeStruct(basis.shape, f3...  0.9 us

profile of v2, /device:TPU:0, one launch (start us, length us, event | category | flops | bytes accessed | tf_op | source)
XLA Modules:
  0.0 23.4 jit_solution(5420368691269441559)
XLA Ops:
  0.6 21.9 %shard_map.41 = (f32[6,8,32,128]{3,2,1,0:T(8,128)S(1)}, f32[2,5]{1,0:T(2,128)S(1)}) custom-call(f32[8,32,128]{2,1,0:T(8,128)} %x_hbm.1, f32[8,32,128]{2,1,0:T(8,128)} %pot_hbm.1), custom_call_target="tpu_custom_call" | custom-call | tf_op jit(solution)/shard_map/pallas_call | solution.py:501
  22.5 0.9 %shard_map.42 = (f32[6,8,32,128]{3,2,1,0:T(8,128)}, f32[2,5]{1,0:T(2,128)}) custom-call(f32[6,8,32,128]{3,2,1,0:T(8,128)S(1)} %get-tuple-element.4.basis_ref, f32[2,5]{1,0:T(2,128)S(1)} %get-tuple-element.5.tri_ref), custom_call_target="tpu_custom_call" | custom-call | tf_op jit(solution)/shard_map/pallas_call | solution.py:529

commit v3 on v2

--- a/solution.py
+++ b/solution.py
@@ -18,7 +18,7 @@
 LEAST_SQUARE, MOST_SQUARE = 0.25, 40.0
 LEAST_SHIFT, MOST_SHIFT = 0.5, 16.5
 VECTOR, POTENTIAL = 0, 1
-RELAY_RING, RELAY_WAVE = 4, 4
+RELAY_RING, RELAYED = 4, 5
 
 
 def times(coeff, columns):
@@ -176,8 +176,8 @@
             ref.at[core, lands(side, d), rows(step, count, False)],
             send_sem.at[i, t], recv_sem.at[i, core], (t, py - step, pz - q))
 
-    relays = [(a, d) for w in range(RELAY_WAVE, D + 1) for a, d in ((VECTOR, w), (POTENTIAL, w - 1))] if (
-        B == RELAY_RING and plane_of(0, 0, D)[0] == -1) else []
+    order = [(a, d) for w in range(1, D + 1) for a, d in ((VECTOR, w), (POTENTIAL, w - 1)) if d]
+    relays = order[-RELAYED:] if B == RELAY_RING and plane_of(0, 0, D)[0] == -1 else []
 
     def relay_copy(k, t):
         array, d = relays[k]
@@ -208,14 +208,15 @@
                     sign = -1 if sending else 1
                     own = None if sending else slab == t
 
-                    def straight(t=t, side=side, mine=mine):
-                        for array, d in mine:
-                            act(array, t, side, d, 0)
-
-                    direct = None
-                    if sending and t == side and set(mine) & set(relays):
-                        direct = pz != 1 + t
-                    guarded([own, within(sign * q, pz, B), direct], straight)
+                    for turned in (False, True):
+                        some = [key for key in mine
+                                if (sending and t == side and key in relays) == turned]
+                        if some:
+                            def straight(t=t, side=side, some=some):
+                                for array, d in some:
+                                    act(array, t, side, d, 0)
+
+                            guarded([own, within(sign * q, pz, B), pz != 1 + t if turned else None], straight)
                     for step in (-1, 1):
                         beside = [(a, d) for a, d in mine if reach(a) > d]
                         if beside:
@@ -389,18 +390,37 @@
     lane = lax.broadcasted_iota(jnp.int32, (YE, X), 1)
     low_rows, high_rows = (py > 0).astype(jnp.float32), (py < A - 1).astype(jnp.float32)
 
-    def level(l, e):
+    def depth(e):
+        return max(D - e, e - (D + H - 1))
+
+    def outer(e):
+        return [b for b in (e - 1, e + 1) if depth(b) > depth(e)]
+
+    def prepare(l, e):
         left, right = cells[l - 1, 0, e], cells[l - 1, 1, e]
         up = [pltpu.roll(v, 1, 1) for v in (left, right)]
         down = [pltpu.roll(v, X - 1, 1) for v in (left, right)]
         along = (jnp.where(lane == 0, 0.0, up[0]) + jnp.where(lane == X - 1, down[1], down[0]),
                  jnp.where(lane == 0, up[0], up[1]) + jnp.where(lane == X - 1, 0.0, down[1]))
         for core, here in enumerate((left, right)):
-            around = (cells[l - 1, core, e - 1] + cells[l - 1, core, e + 1]
-                      + (pltpu.roll(here, 1, 0) + pltpu.roll(here, YE - 1, 0)) + along[core])
-            image = ((DIAGONAL - shifts[l - 1]) + ext[core, e]) * here - around
-            if taus[l - 1] is not None:
+            around = (pltpu.roll(here, 1, 0) + pltpu.roll(here, YE - 1, 0)) + along[core]
+            for b in (e - 1, e + 1):
+                if b not in outer(e):
+                    around = around + cells[l - 1, core, b]
+            if l == 1:
+                image = -around
+            else:
+                image = ((DIAGONAL - shifts[l - 1]) + ext[core, e]) * here - around
                 image = image - taus[l - 1] * cells[l - 2, core, e]
+            cells[l, core, e] = image
+
+    def finish(l, e):
+        for core in range(2):
+            image = cells[l, core, e]
+            for b in outer(e):
+                image = image - cells[l - 1, core, b]
+            if l == 1:
+                image = ((DIAGONAL - shifts[0]) + ext[core, e]) * cells[0, core, e] + image
             if not D <= e < D + H:
                 image = image * present[e].astype(jnp.float32)
             cells[l, core, e, inside] = image[T:T + Y]
@@ -408,10 +428,13 @@
                 cells[l, core, e, 0:T] = image[0:T] * low_rows
                 cells[l, core, e, T + Y:YE] = image[T + Y:YE] * high_rows
 
-    def measure(pairs):
-        sums = [jnp.zeros((T, X), jnp.float32)] * len(pairs)
+    def wave(w):
+        return [(l, e) for l in range(1, D + 1) for e in range(l, ZE - l) if max(l + depth(e), 0) == w]
+
+    def measure(pairs, at, sums=None):
+        sums = sums or [jnp.zeros((T, X), jnp.float32)] * len(pairs)
         for core in range(2):
-            for e in range(D, D + H):
+            for e in at:
                 held = {k: cells[k, core, e, inside] for k in sorted({k for pair in pairs for k in pair})}
                 for i, (k, l) in enumerate(pairs):
                     sums[i] = sums[i] + fold(held[k] * held[l])
@@ -422,18 +445,25 @@
     sides(False, lambda array, core, step: side_arrival(array, core, step).wait_recv())
     early = [(k, l) for l in range(D) for k in range(l + 1)]
     late = [(k, D) for k in range(D + 1)]
-    for w in range(D + 1):
-        if w:
-            planes(w, False, take_plane)
-        for l in range(1, D + 1):
-            for e in range(l, ZE - l):
-                if l + max(D - e, e - (D + H - 1)) == w:
-                    level(l, e)
-        if 1 <= w:
-            swap_copy(w).start()
+    held = range(D, D + H)
+    done = [e for e in held if depth(e) < 0]
+    for l, e in wave(0):
+        prepare(l, e)
+        finish(l, e)
+    for l, e in wave(1):
+        prepare(l, e)
+    for w in range(1, D + 1):
+        planes(w, False, take_plane)
+        for l, e in wave(w):
+            finish(l, e)
+        swap_copy(w).start()
         if w == D - 1:
-            sums = measure(early)
-    sums = sums + measure(late)
+            sums = measure(early, held)
+            last = measure(late, done)
+        if w < D:
+            for l, e in wave(w + 1):
+                prepare(l, e)
+    sums = sums + measure(late, [e for e in held if e not in done], last)
     share(1, sums)
     to_others(lambda target: stat_copy(1, target).start())
     stats = gathered(1, len(sums))
@@ -507,13 +537,13 @@
             pltpu.VMEM((D + 1,) + extended, f32),
             pltpu.VMEM(extended, f32),
             pltpu.VMEM((D, H, Y, X), f32),
-            pltpu.VMEM((2 * (D + 1 - RELAY_WAVE), Y, X), f32),
+            pltpu.VMEM((RELAYED, Y, X), f32),
             pltpu.VMEM((2, n, 1, X), f32),
             dma((2 * 2 * D * 3, 2)),
             dma((2 * 2 * D * 3, 2)),
-            dma((2 * (D + 1 - RELAY_WAVE),)),
-            dma((2 * (D + 1 - RELAY_WAVE),)),
-            dma((2 * (D + 1 - RELAY_WAVE),)),
+            dma((RELAYED,)),
+            dma((RELAYED,)),
+            dma((RELAYED,)),
             dma((2, 2, 2)),
             dma((2, 2, 2)),
             dma((2,)),

time: 23.6 us -> 23 us (0.975)
  Pallas kernels: 22.8 us -> 22.3 us
    pallas_call x1, Pallas kernels: 21.9 us -> 21.4 us  [shards(): pl.pallas_call(functools.partial(kernel, sizes, 1.0 / (start_vector.size...]
where the time goes in v3:
time: 23 us; the launch traced here: 22.9 us
  Pallas kernels  22.3 us (97%)
  between operations  0.64 us (3%)
    pallas_call x1, Pallas kernels, shards(): pl.pallas_call(functools.partial(kernel, sizes, 1.0 / (start_vector.size...  21.4 us
    pallas_call x1, Pallas kernels, shards(): pl.pallas_call(write_out, out_shape=(jax.ShapeDtypeStruct(basis.shape, f3...  0.9 us

profile of v3, /device:TPU:0, one launch (start us, length us, event | category | flops | bytes accessed | tf_op | source)
XLA Modules:
  0.0 22.9 jit_solution(17136015724988135427)
XLA Ops:
  0.6 21.4 %shard_map.41 = (f32[6,8,32,128]{3,2,1,0:T(8,128)S(1)}, f32[2,5]{1,0:T(2,128)S(1)}) custom-call(f32[8,32,128]{2,1,0:T(8,128)} %x_hbm.1, f32[8,32,128]{2,1,0:T(8,128)} %pot_hbm.1), custom_call_target="tpu_custom_call" | custom-call | tf_op jit(solution)/shard_map/pallas_call | solution.py:531
  22.0 0.9 %shard_map.42 = (f32[6,8,32,128]{3,2,1,0:T(8,128)}, f32[2,5]{1,0:T(2,128)}) custom-call(f32[6,8,32,128]{3,2,1,0:T(8,128)S(1)} %get-tuple-element.4.basis_ref, f32[2,5]{1,0:T(2,128)S(1)} %get-tuple-element.5.tri_ref), custom_call_target="tpu_custom_call" | custom-call | tf_op jit(solution)/shard_map/pallas_call | solution.py:559

commit v4 on v3

--- a/solution.py
+++ b/solution.py
@@ -19,6 +19,7 @@
 LEAST_SHIFT, MOST_SHIFT = 0.5, 16.5
 VECTOR, POTENTIAL = 0, 1
 RELAY_RING, RELAYED = 4, 5
+CHUNK = 3
 
 
 def times(coeff, columns):
@@ -92,8 +93,8 @@
 
 
 def kernel(sizes, per_cell, x_hbm, pot_hbm, out_ref, tri_ref, cells, ext, swapped, relayed, slots,
-           send_sem, recv_sem, relay_send, relay_recv, onward_send, side_send, side_recv, near_send, near_recv, swap_send, swap_recv,
-           stat_send, stat_recv, load_sem):
+           group_send, plane_recv, corner_recv, relay_recv, relay_send, side_send, side_recv,
+           pair_send, pair_recv, stat_send, stat_recv, load_sem):
     Z, Y, X = x_hbm.shape
     S, A, B = sizes
     n = S * A * B
@@ -150,8 +151,7 @@
             pl.when(functools.reduce(jnp.logical_and, conditions))(act)
 
     def plane_of(t, side, d):
-        z = t * H - d if side == 0 else t * H + H - 1 + d
-        return z // Z, z % Z
+        return block_of(t, side, d, Z)
 
     def lands(side, d):
         return D - d if side == 0 else D + H - 1 + d
@@ -163,32 +163,40 @@
             return pl.ds(T + Y - count, count) if sending else pl.ds(T - count, count)
         return pl.ds(T, count) if sending else pl.ds(T + Y, count)
 
-    def index(array, side, d, step):
-        return ((array * 2 + side) * D + d - 1) * 3 + step + 1
-
-    def plane_copy(array, t, side, d, step, core):
+    def arrival(array, side, d, step):
+        w = d if array == VECTOR else d + 1
+        return plane_recv.at[side, w - 1] if step == 0 else corner_recv.at[side, w - 1, step > 0 and 1 or 0]
+
+    def plane_copy(array, t, side, d, step, sent):
         q, z = plane_of(t, side, d)
         count = reach(array) - d
         ref = source(array)
-        i = index(array, side, d, step)
         return remote(
-            ref.at[core, z + first_plane, rows(step, count, True)],
-            ref.at[core, lands(side, d), rows(step, count, False)],
-            send_sem.at[i, t], recv_sem.at[i, core], (t, py - step, pz - q))
+            ref.at[slab, z + first_plane, rows(step, count, True)],
+            ref.at[slab, lands(side, d), rows(step, count, False)],
+            sent, arrival(array, side, d, step), (t, py - step, pz - q))
+
+    def wait_for(span, sem):
+        pltpu.make_async_copy(span, span, sem).wait()
+
+    def lines(count):
+        if count % Y == 0:
+            return cells.at[0, 0, pl.ds(0, count // Y), pl.ds(0, Y)]
+        return cells.at[0, 0, 0, pl.ds(0, count)]
 
     order = [(a, d) for w in range(1, D + 1) for a, d in ((VECTOR, w), (POTENTIAL, w - 1)) if d]
-    relays = order[-RELAYED:] if B == RELAY_RING and plane_of(0, 0, D)[0] == -1 else []
+    relays = order[-RELAYED:] if relaying(Z, B) else []
 
     def relay_copy(k, t):
         array, d = relays[k]
         z = plane_of(t, t, d)[1]
         return remote(source(array).at[slab, z + first_plane, inside], relayed.at[k],
-                      relay_send.at[k], relay_recv.at[k], (slab, py, B - 1 if t == 0 else 0))
+                      relay_send.at[0], relay_recv.at[k], (slab, py, B - 1 if t == 0 else 0))
 
     def onward_copy(k, t):
         array, d = relays[k]
-        return remote(relayed.at[k], source(array).at[slab, lands(t, d), inside], onward_send.at[k],
-                      recv_sem.at[index(array, t, d, 0), slab], (t, py, B - 2 if t == 0 else 1))
+        return remote(relayed.at[k], source(array).at[slab, lands(t, d), inside], relay_send.at[1],
+                      arrival(array, t, d, 0), (t, py, B - 2 if t == 0 else 1))
 
     def each_relay(at, act):
         for t in range(2):
@@ -198,7 +206,8 @@
                     for k in range(len(relays)):
                         act(k, t)
 
-    def planes(w, sending, act):
+    def batches(w, sending):
+        found = []
         for t in range(2):
             for side in range(2):
                 wanted = [(array, d) for array, d in ((VECTOR, w), (POTENTIAL, w - 1))
@@ -206,75 +215,80 @@
                 for q in sorted({plane_of(t, side, d)[0] for _, d in wanted}, key=abs):
                     mine = [(a, d) for a, d in wanted if plane_of(t, side, d)[0] == q]
                     sign = -1 if sending else 1
-                    own = None if sending else slab == t
-
+                    there = [None if sending else slab == t, within(sign * q, pz, B)]
                     for turned in (False, True):
-                        some = [key for key in mine
-                                if (sending and t == side and key in relays) == turned]
-                        if some:
-                            def straight(t=t, side=side, some=some):
-                                for array, d in some:
-                                    act(array, t, side, d, 0)
-
-                            guarded([own, within(sign * q, pz, B), pz != 1 + t if turned else None], straight)
+                        keys = [(a, t, side, d, 0) for a, d in mine
+                                if (sending and t == side and (a, d) in relays) == turned]
+                        found.append(((t, side, q, 0, turned), there + [pz != 1 + t if turned else None], keys))
                     for step in (-1, 1):
-                        beside = [(a, d) for a, d in mine if reach(a) > d]
-                        if beside:
-                            def corner(t=t, side=side, beside=beside, step=step):
-                                for array, d in beside:
-                                    act(array, t, side, d, step)
-
-                            guarded([own, within(sign * q, pz, B), within(sign * step, py, A)], corner)
-
-    def start_plane(*key):
-        plane_copy(*key, slab).start()
-
-    def finish_plane(*key):
-        plane_copy(*key, slab).wait_send()
-
-    def take_plane(*key):
-        for core in range(2):
-            plane_copy(*key, core).wait_recv()
-
-    def side_copy(array, t, step, core):
+                        keys = [(a, t, side, d, step) for a, d in mine if reach(a) > d]
+                        found.append(((t, side, q, step, False), there + [within(sign * step, py, A)], keys))
+        return [batch for batch in found if batch[2]]
+
+    def volume(keys):
+        return sum(Y if step == 0 else reach(array) - d for array, _, _, d, step in keys)
+
+    groups = {}
+    for w in range(1, D + 1):
+        for tag, conditions, keys in batches(w, True):
+            _, _, size = groups.get(tag, (0, 0, 0))
+            groups[tag] = (conditions, list(groups).index(tag) if tag in groups else len(groups), size + volume(keys))
+
+    assert len(groups) == group_count(Z, B)
+
+    def send_planes(w):
+        for tag, conditions, keys in batches(w, True):
+            def start(tag=tag, keys=keys):
+                for key in keys:
+                    plane_copy(*key, group_send.at[groups[tag][1]]).start()
+            guarded(conditions, start)
+
+    def finish_planes():
+        for conditions, g, size in groups.values():
+            guarded(conditions, lambda g=g, size=size: wait_for(lines(size), group_send.at[g]))
+
+    def take_planes(w):
+        for tag, conditions, keys in batches(w, False):
+            array, _, side, d, step = keys[0]
+            guarded(conditions, lambda keys=keys, sem=arrival(array, side, d, step): wait_for(
+                lines(2 * volume(keys)), sem))
+
+    def side_copy(array, t, step):
         ref = source(array)
         count = reach(array)
+        k = step > 0 and 1 or 0
         return remote(
-            ref.at[core, pl.ds(first_plane, Z), rows(step, count, True)],
-            ref.at[core, pl.ds(D - t * H, Z), rows(step, count, False)],
-            side_send.at[array, step > 0 and 1 or 0, t], side_recv.at[array, step > 0 and 1 or 0, core],
-            (t, py - step, pz))
-
-    def sides(sending, act):
+            ref.at[slab, pl.ds(first_plane, Z), rows(step, count, True)],
+            ref.at[slab, pl.ds(D - t * H, Z), rows(step, count, False)],
+            side_send.at[k], side_recv.at[k], (t, py - step, pz))
+
+    def send_sides():
         for step in (-1, 1):
             def both(step=step):
                 for array in (VECTOR, POTENTIAL):
                     for other in range(2):
-                        act(array, other, step)
-            guarded([within(-step if sending else step, py, A)], both)
+                        side_copy(array, other, step).start()
+            guarded([within(-step, py, A)], both)
+
+    def wait_sides(sign, sems):
+        span = cells.at[0, 0, pl.ds(0, Z), pl.ds(0, 2 * (reach(VECTOR) + reach(POTENTIAL)))]
+        for k, step in enumerate((-1, 1)):
+            guarded([within(sign * step, py, A)], lambda k=k: wait_for(span, sems.at[k]))
 
     def near_copy(array):
         ref = source(array)
         return remote(
             ref.at[slab, pl.ds(first_plane, Z), inside],
             ref.at[slab, pl.ds(D - (1 - slab) * H, Z), inside],
-            near_send.at[array], near_recv.at[array], partner)
-
-    def near_arrival(array):
-        ref = source(array)
-        span = ref.at[1 - slab, pl.ds(first_plane, Z), inside]
-        return remote(span, span, near_send.at[array], near_recv.at[array], partner)
-
-    def side_arrival(array, core, step):
-        ref = source(array)
-        span = ref.at[core, pl.ds(first_plane, Z), rows(step, reach(array), False)]
-        k = step > 0 and 1 or 0
-        return remote(span, span, side_send.at[array, k, 0], side_recv.at[array, k, core], partner)
+            pair_send.at[0], pair_recv.at[0], partner)
+
+    def wait_near(sem):
+        wait_for(cells.at[0, pl.ds(0, 2), pl.ds(0, Z), pl.ds(0, Y)], sem)
 
     def swap_copy(level):
         return remote(
             cells.at[level, 1 - slab, pl.ds(D, H), inside], swapped.at[level - 1],
-            swap_send.at[level - 1], swap_recv.at[level - 1], partner)
+            pair_send.at[1], pair_recv.at[1], partner)
 
     def stat_copy(p, target):
         return remote(slots.at[p, me], slots.at[p, me], stat_send.at[p], stat_recv.at[p], target)
@@ -361,10 +375,10 @@
     each_relay((1, 2), lambda k, t: relay_copy(k, t).start())
     for array in (VECTOR, POTENTIAL):
         near_copy(array).start()
-    planes(1, True, start_plane)
-    sides(True, lambda array, t, step: side_copy(array, t, step, slab).start())
+    send_planes(1)
+    send_sides()
     for w in range(2, D + 1):
-        planes(w, True, start_plane)
+        send_planes(w)
 
     def forward(k, t):
         relay_copy(k, t).wait_recv()
@@ -387,8 +401,17 @@
     shifts = [alpha[0]] + [alpha[1]] * (D - 1)
     taus = [None, square[0]] + [square[1]] * (D - 2)
 
-    lane = lax.broadcasted_iota(jnp.int32, (YE, X), 1)
-    low_rows, high_rows = (py > 0).astype(jnp.float32), (py < A - 1).astype(jnp.float32)
+    first_lane = lax.broadcasted_iota(jnp.int32, (T, X), 1) == 0
+    last_lane = lax.broadcasted_iota(jnp.int32, (T, X), 1) == X - 1
+    line = lax.broadcasted_iota(jnp.int32, (T, X), 0)
+    low_rows = jnp.where(jnp.logical_and(line < D - 1, py == 0), 0.0, 1.0)
+    high_rows = jnp.where(jnp.logical_and(line > T - D, py == A - 1), 0.0, 1.0)
+
+    def windows(l):
+        reach = D - 1 if l < D else 0
+        count = (Y + 2 * reach) // T
+        starts = [T - reach + T * i for i in range(count)]
+        return [(starts[i], min(CHUNK, count - i), i) for i in range(0, count, CHUNK)], count
 
     def depth(e):
         return max(D - e, e - (D + H - 1))
@@ -396,37 +419,49 @@
     def outer(e):
         return [b for b in (e - 1, e + 1) if depth(b) > depth(e)]
 
+    def tiled(mask, tiles):
+        return jnp.concatenate([mask] * tiles, axis=0) if tiles > 1 else mask
+
     def prepare(l, e):
-        left, right = cells[l - 1, 0, e], cells[l - 1, 1, e]
-        up = [pltpu.roll(v, 1, 1) for v in (left, right)]
-        down = [pltpu.roll(v, X - 1, 1) for v in (left, right)]
-        along = (jnp.where(lane == 0, 0.0, up[0]) + jnp.where(lane == X - 1, down[1], down[0]),
-                 jnp.where(lane == 0, up[0], up[1]) + jnp.where(lane == X - 1, 0.0, down[1]))
-        for core, here in enumerate((left, right)):
-            around = (pltpu.roll(here, 1, 0) + pltpu.roll(here, YE - 1, 0)) + along[core]
-            for b in (e - 1, e + 1):
-                if b not in outer(e):
-                    around = around + cells[l - 1, core, b]
-            if l == 1:
-                image = -around
-            else:
-                image = ((DIAGONAL - shifts[l - 1]) + ext[core, e]) * here - around
-                image = image - taus[l - 1] * cells[l - 2, core, e]
-            cells[l, core, e] = image
+        for start, tiles, _ in windows(l)[0]:
+            at = lambda shift=0: pl.ds(start + shift, tiles * T)
+            left, right = cells[l - 1, 0, e, at()], cells[l - 1, 1, e, at()]
+            up = [pltpu.roll(v, 1, 1) for v in (left, right)]
+            down = [pltpu.roll(v, X - 1, 1) for v in (left, right)]
+            head, tail = tiled(first_lane, tiles), tiled(last_lane, tiles)
+            along = (jnp.where(head, 0.0, up[0]) + jnp.where(tail, down[1], down[0]),
+                     jnp.where(head, up[0], up[1]) + jnp.where(tail, 0.0, down[1]))
+            for core, here in enumerate((left, right)):
+                around = (cells[l - 1, core, e, at(-1)] + cells[l - 1, core, e, at(1)]) + along[core]
+                for b in (e - 1, e + 1):
+                    if b not in outer(e):
+                        around = around + cells[l - 1, core, b, at()]
+                if l == 1:
+                    image = -around
+                else:
+                    image = ((DIAGONAL - shifts[l - 1]) + ext[core, e, at()]) * here - around
+                    image = image - taus[l - 1] * cells[l - 2, core, e, at()]
+                cells[l, core, e, at()] = image
 
     def finish(l, e):
+        chunks, count = windows(l)
         for core in range(2):
-            image = cells[l, core, e]
-            for b in outer(e):
-                image = image - cells[l - 1, core, b]
-            if l == 1:
-                image = ((DIAGONAL - shifts[0]) + ext[core, e]) * cells[0, core, e] + image
-            if not D <= e < D + H:
-                image = image * present[e].astype(jnp.float32)
-            cells[l, core, e, inside] = image[T:T + Y]
-            if l < D:
-                cells[l, core, e, 0:T] = image[0:T] * low_rows
-                cells[l, core, e, T + Y:YE] = image[T + Y:YE] * high_rows
+            for start, tiles, first in chunks:
+                at = pl.ds(start, tiles * T)
+                image = cells[l, core, e, at]
+                for b in outer(e):
+                    image = image - cells[l - 1, core, b, at]
+                if l == 1:
+                    image = ((DIAGONAL - shifts[0]) + ext[core, e, at]) * cells[0, core, e, at] + image
+                if not D <= e < D + H:
+                    image = image * present[e].astype(jnp.float32)
+                for i in range(tiles):
+                    part = image[i * T:(i + 1) * T]
+                    if l < D and first + i == 0:
+                        part = part * low_rows
+                    if l < D and first + i == count - 1:
+                        part = part * high_rows
+                    cells[l, core, e, pl.ds(start + i * T, T)] = part
 
     def wave(w):
         return [(l, e) for l in range(1, D + 1) for e in range(l, ZE - l) if max(l + depth(e), 0) == w]
@@ -440,9 +475,8 @@
                     sums[i] = sums[i] + fold(held[k] * held[l])
         return sums
 
-    for array in (VECTOR, POTENTIAL):
-        near_arrival(array).wait_recv()
-    sides(False, lambda array, core, step: side_arrival(array, core, step).wait_recv())
+    wait_near(pair_recv.at[0])
+    wait_sides(1, side_recv)
     early = [(k, l) for l in range(D) for k in range(l + 1)]
     late = [(k, D) for k in range(D + 1)]
     held = range(D, D + H)
@@ -453,7 +487,7 @@
     for l, e in wave(1):
         prepare(l, e)
     for w in range(1, D + 1):
-        planes(w, False, take_plane)
+        take_planes(w)
         for l, e in wave(w):
             finish(l, e)
         swap_copy(w).start()
@@ -466,6 +500,17 @@
     sums = sums + measure(late, [e for e in held if e not in done], last)
     share(1, sums)
     to_others(lambda target: stat_copy(1, target).start())
+    wait_near(pair_send.at[0])
+    wait_sides(-1, side_send)
+    if relays:
+        for at, k in (((1, 2), 0), ((B - 1, 0), 1)):
+            @pl.when(jnp.logical_or(pz == at[0], pz == at[1]))
+            def _(k=k):
+                wait_for(relayed, relay_send.at[k])
+    finish_planes()
+    wait_for(swapped, pair_send.at[1])
+    wait_all(0, stat_send.at[0])
+    wait_for(swapped, pair_recv.at[1])
     stats = gathered(1, len(sums))
     scale = 1.0 / jnp.sqrt(stats[0] + EPSILON)
     inner = {}
@@ -478,8 +523,6 @@
         tri_ref[1:2, v:v + 1] = betas[v][:, 0:1]
     found = [{q: t * scale for q, t in coords.items()} for coords in found]
 
-    for l in range(1, D + 1):
-        swap_copy(l).wait_recv()
     for half in range(2):
         for i in range(H):
             if half == 0:
@@ -496,17 +539,25 @@
                     total = term if total is None else total + term
                 out_ref[k + 1, z] = total
 
-    for array in (VECTOR, POTENTIAL):
-        near_copy(array).wait_send()
-    sides(True, lambda array, t, step: side_copy(array, t, step, slab).wait_send())
-    each_relay((1, 2), lambda k, t: relay_copy(k, t).wait_send())
-    each_relay((B - 1, 0), lambda k, t: onward_copy(k, t).wait_send())
-    for w in range(1, D + 1):
-        planes(w, True, finish_plane)
-    for l in range(1, D + 1):
-        swap_copy(l).wait_send()
-    for p in range(2):
-        wait_all(p, stat_send.at[p])
+    wait_all(1, stat_send.at[1])
+
+
+def block_of(t, side, d, Z):
+    z = t * (Z // 2) - d if side == 0 else (t + 1) * (Z // 2) - 1 + d
+    return z // Z, z % Z
+
+
+def relaying(Z, B):
+    return B == RELAY_RING and block_of(0, 0, ITERS, Z)[0] == -1
+
+
+def group_count(Z, B):
+    count = 2 if relaying(Z, B) else 0
+    for t in range(2):
+        for side in range(2):
+            blocks = [block_of(t, side, d, Z)[0] for d in range(1, ITERS + 1)]
+            count += len(set(blocks) - {0}) + 2 * len(set(blocks[:-1]) - {0})
+    return count
 
 
 def write_out(basis_ref, tri_ref, basis_out, tri_out, sems):
@@ -539,17 +590,15 @@
             pltpu.VMEM((D, H, Y, X), f32),
             pltpu.VMEM((RELAYED, Y, X), f32),
             pltpu.VMEM((2, n, 1, X), f32),
-            dma((2 * 2 * D * 3, 2)),
-            dma((2 * 2 * D * 3, 2)),
+            dma((group_count(Z, sizes[2]),)),
+            dma((2, D)),
+            dma((2, D - 1, 2)),
             dma((RELAYED,)),
-            dma((RELAYED,)),
-            dma((RELAYED,)),
-            dma((2, 2, 2)),
-            dma((2, 2, 2)),
-            dma((2,)),
-            dma((2,)),
-            dma((D,)),
-            dma((D,)),
+            dma((2,)),
+            dma((2,)),
+            dma((2,)),
+            dma((2,)),
+            dma((2,)),
             dma((2,)),
             dma((2,)),
             dma((2,)),

time: 23 us -> 20.7 us (0.900)
  Pallas kernels: 22.3 us -> 19.9 us
    pallas_call x1, Pallas kernels: 21.4 us -> 19 us  [shards(): pl.pallas_call(functools.partial(kernel, sizes, 1.0 / (start_vector.size...]
where the time goes in v4:
time: 20.7 us; the launch traced here: 20.5 us
  Pallas kernels  19.9 us (96%)
  between operations  0.64 us (3%)
    pallas_call x1, Pallas kernels, shards(): pl.pallas_call(functools.partial(kernel, sizes, 1.0 / (start_vector.size...  19 us
    pallas_call x1, Pallas kernels, shards(): pl.pallas_call(write_out, out_shape=(jax.ShapeDtypeStruct(basis.shape, f3...  0.9 us

profile of v4, /device:TPU:0, one launch (start us, length us, event | category | flops | bytes accessed | tf_op | source)
XLA Modules:
  0.0 20.5 jit_solution(15525649369777375447)
XLA Ops:
  0.6 19.0 %shard_map.41 = (f32[6,8,32,128]{3,2,1,0:T(8,128)S(1)}, f32[2,5]{1,0:T(2,128)S(1)}) custom-call(f32[8,32,128]{2,1,0:T(8,128)} %x_hbm.1, f32[8,32,128]{2,1,0:T(8,128)} %pot_hbm.1), custom_call_target="tpu_custom_call" | custom-call | tf_op jit(solution)/shard_map/pallas_call | solution.py:582
  19.6 0.9 %shard_map.42 = (f32[6,8,32,128]{3,2,1,0:T(8,128)}, f32[2,5]{1,0:T(2,128)}) custom-call(f32[6,8,32,128]{3,2,1,0:T(8,128)S(1)} %get-tuple-element.4.basis_ref, f32[2,5]{1,0:T(2,128)S(1)} %get-tuple-element.5.tri_ref), custom_call_target="tpu_custom_call" | custom-call | tf_op jit(solution)/shard_map/pallas_call | solution.py:608

commit v5 on v4

--- a/solution.py
+++ b/solution.py
@@ -93,8 +93,7 @@
 
 
 def kernel(sizes, per_cell, x_hbm, pot_hbm, out_ref, tri_ref, cells, ext, swapped, relayed, slots,
-           group_send, plane_recv, corner_recv, relay_recv, relay_send, side_send, side_recv,
-           pair_send, pair_recv, stat_send, stat_recv, load_sem):
+           group_send, plane_recv, corner_recv, relay_recv, relay_send, side_sems, pair_sems, stat_sems, load_sem):
     Z, Y, X = x_hbm.shape
     S, A, B = sizes
     n = S * A * B
@@ -163,9 +162,11 @@
             return pl.ds(T + Y - count, count) if sending else pl.ds(T - count, count)
         return pl.ds(T, count) if sending else pl.ds(T + Y, count)
 
-    def arrival(array, side, d, step):
+    def arrival(array, t, side, d, step):
         w = d if array == VECTOR else d + 1
-        return plane_recv.at[side, w - 1] if step == 0 else corner_recv.at[side, w - 1, step > 0 and 1 or 0]
+        if side != t:
+            w = w + H - Z + (D if step == 0 else D - 1)
+        return (plane_recv if step == 0 else corner_recv).at[w - 1]
 
     def plane_copy(array, t, side, d, step, sent):
         q, z = plane_of(t, side, d)
@@ -174,15 +175,20 @@
         return remote(
             ref.at[slab, z + first_plane, rows(step, count, True)],
             ref.at[slab, lands(side, d), rows(step, count, False)],
-            sent, arrival(array, side, d, step), (t, py - step, pz - q))
+            sent, arrival(array, t, side, d, step), (t, py - step, pz - q))
 
     def wait_for(span, sem):
         pltpu.make_async_copy(span, span, sem).wait()
 
     def lines(count):
-        if count % Y == 0:
-            return cells.at[0, 0, pl.ds(0, count // Y), pl.ds(0, Y)]
-        return cells.at[0, 0, 0, pl.ds(0, count)]
+        if count % Y:
+            return cells.at[0, 0, 0, pl.ds(0, count)]
+        a, b, c = next((a, b, count // Y // (a * b)) for a in range(1, D + 2) for b in (1, 2)
+                       if count // Y % (a * b) == 0 and count // Y // (a * b) <= ZE)
+        return cells.at[pl.ds(0, a), pl.ds(0, b), pl.ds(0, c), pl.ds(0, Y)]
+
+    below, above = py > 0, py < A - 1
+    beside_both, beside_one = jnp.logical_and(below, above), below != above
 
     order = [(a, d) for w in range(1, D + 1) for a, d in ((VECTOR, w), (POTENTIAL, w - 1)) if d]
     relays = order[-RELAYED:] if relaying(Z, B) else []
@@ -195,8 +201,8 @@
 
     def onward_copy(k, t):
         array, d = relays[k]
-        return remote(relayed.at[k], source(array).at[slab, lands(t, d), inside], relay_send.at[1],
-                      arrival(array, t, d, 0), (t, py, B - 2 if t == 0 else 1))
+        return remote(relayed.at[k], source(array).at[slab, lands(t, d), inside], relay_send.at[0],
+                      arrival(array, t, t, d, 0), (t, py, B - 2 if t == 0 else 1))
 
     def each_relay(at, act):
         for t in range(2):
@@ -219,48 +225,60 @@
                     for turned in (False, True):
                         keys = [(a, t, side, d, 0) for a, d in mine
                                 if (sending and t == side and (a, d) in relays) == turned]
-                        found.append(((t, side, q, 0, turned), there + [pz != 1 + t if turned else None], keys))
-                    for step in (-1, 1):
-                        keys = [(a, t, side, d, step) for a, d in mine if reach(a) > d]
-                        found.append(((t, side, q, step, False), there + [within(sign * step, py, A)], keys))
+                        found.append(((q, 0, turned), there + [pz != 1 + t if turned else None], keys))
+                    low, high = ([(a, t, side, d, step) for a, d in mine if reach(a) > d] for step in (-1, 1))
+                    if sending:
+                        found.append(((q, -1, False), there + [above], low))
+                        found.append(((q, 1, False), there + [below], high))
+                    else:
+                        found.append(((q, 1, False), there + [beside_both], low + high))
+                        found.append(((q, 1, False), there + [beside_one], low))
         return [batch for batch in found if batch[2]]
 
     def volume(keys):
         return sum(Y if step == 0 else reach(array) - d for array, _, _, d, step in keys)
 
-    groups = {}
+    totals = {}
     for w in range(1, D + 1):
         for tag, conditions, keys in batches(w, True):
-            _, _, size = groups.get(tag, (0, 0, 0))
-            groups[tag] = (conditions, list(groups).index(tag) if tag in groups else len(groups), size + volume(keys))
-
-    assert len(groups) == group_count(Z, B)
+            totals[tag] = (conditions, totals.get(tag, (0, 0))[1] + volume(keys))
+    slot_of = {tag: i for i, tag in enumerate(dict.fromkeys((q, step and 1, turned) for q, step, turned in totals))}
+    assert len(slot_of) == group_count(Z, B)
+
+    def group(tag):
+        q, step, turned = tag
+        return group_send.at[slot_of[q, step and 1, turned]]
 
     def send_planes(w):
         for tag, conditions, keys in batches(w, True):
             def start(tag=tag, keys=keys):
                 for key in keys:
-                    plane_copy(*key, group_send.at[groups[tag][1]]).start()
+                    plane_copy(*key, group(tag)).start()
             guarded(conditions, start)
 
     def finish_planes():
-        for conditions, g, size in groups.values():
-            guarded(conditions, lambda g=g, size=size: wait_for(lines(size), group_send.at[g]))
+        for tag, (conditions, size) in totals.items():
+            q, step, _ = tag
+            if step == 0:
+                guarded(conditions, lambda tag=tag, size=size: wait_for(lines(size), group(tag)))
+            elif step > 0:
+                for times_, beside in ((2, beside_both), (1, beside_one)):
+                    guarded([within(-q, pz, B), beside], lambda tag=tag, rows_=times_ * size: wait_for(
+                        lines(rows_), group(tag)))
 
     def take_planes(w):
         for tag, conditions, keys in batches(w, False):
-            array, _, side, d, step = keys[0]
-            guarded(conditions, lambda keys=keys, sem=arrival(array, side, d, step): wait_for(
+            array, t, side, d, step = keys[0]
+            guarded(conditions, lambda keys=keys, sem=arrival(array, t, side, d, step): wait_for(
                 lines(2 * volume(keys)), sem))
 
     def side_copy(array, t, step):
         ref = source(array)
         count = reach(array)
-        k = step > 0 and 1 or 0
         return remote(
             ref.at[slab, pl.ds(first_plane, Z), rows(step, count, True)],
             ref.at[slab, pl.ds(D - t * H, Z), rows(step, count, False)],
-            side_send.at[k], side_recv.at[k], (t, py - step, pz))
+            side_sems.at[0], side_sems.at[1], (t, py - step, pz))
 
     def send_sides():
         for step in (-1, 1):
@@ -270,32 +288,26 @@
                         side_copy(array, other, step).start()
             guarded([within(-step, py, A)], both)
 
-    def wait_sides(sign, sems):
-        span = cells.at[0, 0, pl.ds(0, Z), pl.ds(0, 2 * (reach(VECTOR) + reach(POTENTIAL)))]
-        for k, step in enumerate((-1, 1)):
-            guarded([within(sign * step, py, A)], lambda k=k: wait_for(span, sems.at[k]))
+    def wait_sides(sem):
+        count = 2 * (reach(VECTOR) + reach(POTENTIAL))
+        for times_, beside in ((2, beside_both), (1, beside_one)):
+            guarded([beside], lambda times_=times_: wait_for(
+                cells.at[0, 0, pl.ds(0, Z), pl.ds(0, times_ * count)], sem))
 
     def near_copy(array):
         ref = source(array)
         return remote(
             ref.at[slab, pl.ds(first_plane, Z), inside],
             ref.at[slab, pl.ds(D - (1 - slab) * H, Z), inside],
-            pair_send.at[0], pair_recv.at[0], partner)
-
-    def wait_near(sem):
-        wait_for(cells.at[0, pl.ds(0, 2), pl.ds(0, Z), pl.ds(0, Y)], sem)
+            pair_sems.at[0], pair_sems.at[1], partner)
 
     def swap_copy(level):
         return remote(
             cells.at[level, 1 - slab, pl.ds(D, H), inside], swapped.at[level - 1],
-            pair_send.at[1], pair_recv.at[1], partner)
+            pair_sems.at[0], pair_sems.at[2], partner)
 
     def stat_copy(p, target):
-        return remote(slots.at[p, me], slots.at[p, me], stat_send.at[p], stat_recv.at[p], target)
-
-    def wait_all(p, sem):
-        span = slots.at[p, pl.ds(0, n - 1)]
-        pltpu.make_async_copy(span, span, sem).wait()
+        return remote(slots.at[p, me], slots.at[p, me], stat_sems.at[2], stat_sems.at[p], target)
 
     def fold(value):
         return jnp.sum(value.reshape(value.shape[0] // T, T, X), axis=0)
@@ -310,14 +322,14 @@
         slots[p, me] = jnp.sum(jnp.where(at == lanes, totals, 0.0), axis=0, keepdims=True)
 
     def gathered(p, count):
-        wait_all(p, stat_recv.at[p])
+        wait_for(slots.at[p, pl.ds(0, n - 1)], stat_sems.at[p])
         total = jnp.sum(slots[p], axis=0) * per_cell
         return [jnp.broadcast_to(total[:, s:s + 1], (1, X)) for s in range(count)]
 
     barrier = pltpu.get_barrier_semaphore()
     to_others(lambda t: pl.semaphore_signal(barrier, inc=1, device_id=t, device_id_type=MESH))
     loads = [pltpu.make_async_copy(
-        hbm, source(array).at[slab, pl.ds(first_plane, Z), inside], load_sem.at[array])
+        hbm, source(array).at[slab, pl.ds(first_plane, Z), inside], load_sem.at[0])
         for array, hbm in ((VECTOR, x_hbm), (POTENTIAL, pot_hbm))]
     for load in loads:
         load.start()
@@ -339,8 +351,7 @@
                 for core in range(2):
                     for e in range(ZE):
                         ref[core, e, at:at + T] = jnp.zeros((T, X), jnp.float32)
-    for load in loads:
-        load.wait()
+    wait_for(lines(2 * Z * Y), load_sem.at[0])
 
     def rough():
         lane = lax.broadcasted_iota(jnp.int32, (Y, X), 1)
@@ -371,11 +382,11 @@
     share(0, rough())
     pl.semaphore_wait(barrier, n - 1)
 
+    each_relay((1, 2), lambda k, t: relay_copy(k, t).start())
+    send_planes(1)
     to_others(lambda target: stat_copy(0, target).start())
-    each_relay((1, 2), lambda k, t: relay_copy(k, t).start())
     for array in (VECTOR, POTENTIAL):
         near_copy(array).start()
-    send_planes(1)
     send_sides()
     for w in range(2, D + 1):
         send_planes(w)
@@ -385,21 +396,6 @@
         onward_copy(k, t).start()
 
     each_relay((B - 1, 0), forward)
-
-    m0, m1, m2, m3, m4 = gathered(0, 5)
-    some = m0 > 1e-30
-    over = 1.0 / jnp.where(some, m0, 1.0)
-    m1, m2, m3, m4 = m1 * over, m2 * over, m3 * over, m4 * over
-    c2 = m2 - m1 * m1
-    c3 = m3 - 3.0 * m1 * m2 + 2.0 * m1 * m1 * m1
-    c4 = m4 - 4.0 * m1 * m3 + 6.0 * m1 * m1 * m2 - 3.0 * m1 * m1 * m1 * m1
-    down = 1.0 / jnp.maximum(c2, 1e-3)
-    slope = c3 * down
-    bound = lambda value, low, high: jnp.minimum(jnp.maximum(value, low), high)
-    alpha = [bound(jnp.where(some, DIAGONAL + a, CENTER), LEAST_SHIFT, MOST_SHIFT) for a in (m1, m1 + slope)]
-    square = [bound(b, LEAST_SQUARE, MOST_SQUARE) for b in (c2, c4 * down - c2 - slope * slope)]
-    shifts = [alpha[0]] + [alpha[1]] * (D - 1)
-    taus = [None, square[0]] + [square[1]] * (D - 2)
 
     first_lane = lax.broadcasted_iota(jnp.int32, (T, X), 1) == 0
     last_lane = lax.broadcasted_iota(jnp.int32, (T, X), 1) == X - 1
@@ -475,19 +471,48 @@
                     sums[i] = sums[i] + fold(held[k] * held[l])
         return sums
 
-    wait_near(pair_recv.at[0])
-    wait_sides(1, side_recv)
+    wait_for(lines(2 * Z * Y), pair_sems.at[1])
+    wait_sides(side_sems.at[1])
+    ready = []
+    for reached in range(2):
+        if reached:
+            take_planes(reached)
+        for e in range(1, ZE - 1):
+            if depth(e) <= reached and e not in ready:
+                prepare(1, e)
+                ready.append(e)
+
+    m0, m1, m2, m3, m4 = gathered(0, 5)
+    some = m0 > 1e-30
+    over = 1.0 / jnp.where(some, m0, 1.0)
+    m1, m2, m3, m4 = m1 * over, m2 * over, m3 * over, m4 * over
+    c2 = m2 - m1 * m1
+    c3 = m3 - 3.0 * m1 * m2 + 2.0 * m1 * m1 * m1
+    c4 = m4 - 4.0 * m1 * m3 + 6.0 * m1 * m1 * m2 - 3.0 * m1 * m1 * m1 * m1
+    down = 1.0 / jnp.maximum(c2, 1e-3)
+    slope = c3 * down
+    bound = lambda value, low, high: jnp.minimum(jnp.maximum(value, low), high)
+    alpha = [bound(jnp.where(some, DIAGONAL + a, CENTER), LEAST_SHIFT, MOST_SHIFT) for a in (m1, m1 + slope)]
+    square = [bound(b, LEAST_SQUARE, MOST_SQUARE) for b in (c2, c4 * down - c2 - slope * slope)]
+    shifts = [alpha[0]] + [alpha[1]] * (D - 1)
+    taus = [None, square[0]] + [square[1]] * (D - 2)
+
     early = [(k, l) for l in range(D) for k in range(l + 1)]
     late = [(k, D) for k in range(D + 1)]
     held = range(D, D + H)
     done = [e for e in held if depth(e) < 0]
-    for l, e in wave(0):
-        prepare(l, e)
-        finish(l, e)
-    for l, e in wave(1):
-        prepare(l, e)
+    def prepare_all(entries):
+        for l, e in entries:
+            if l > 1 or e not in ready:
+                prepare(l, e)
+
+    for entry in wave(0):
+        prepare_all([entry])
+        finish(*entry)
+    prepare_all(wave(1))
     for w in range(1, D + 1):
-        take_planes(w)
+        if w > 1:
+            take_planes(w)
         for l, e in wave(w):
             finish(l, e)
         swap_copy(w).start()
@@ -495,22 +520,16 @@
             sums = measure(early, held)
             last = measure(late, done)
         if w < D:
-            for l, e in wave(w + 1):
-                prepare(l, e)
+            prepare_all(wave(w + 1))
     sums = sums + measure(late, [e for e in held if e not in done], last)
     share(1, sums)
     to_others(lambda target: stat_copy(1, target).start())
-    wait_near(pair_send.at[0])
-    wait_sides(-1, side_send)
+    wait_for(lines((2 * Z + D * H) * Y), pair_sems.at[0])
+    wait_sides(side_sems.at[0])
     if relays:
-        for at, k in (((1, 2), 0), ((B - 1, 0), 1)):
-            @pl.when(jnp.logical_or(pz == at[0], pz == at[1]))
-            def _(k=k):
-                wait_for(relayed, relay_send.at[k])
+        wait_for(relayed, relay_send.at[0])
     finish_planes()
-    wait_for(swapped, pair_send.at[1])
-    wait_all(0, stat_send.at[0])
-    wait_for(swapped, pair_recv.at[1])
+    wait_for(swapped, pair_sems.at[2])
     stats = gathered(1, len(sums))
     scale = 1.0 / jnp.sqrt(stats[0] + EPSILON)
     inner = {}
@@ -539,7 +558,7 @@
                     total = term if total is None else total + term
                 out_ref[k + 1, z] = total
 
-    wait_all(1, stat_send.at[1])
+    wait_for(slots.at[pl.ds(0, 2), pl.ds(0, n - 1)], stat_sems.at[2])
 
 
 def block_of(t, side, d, Z):
@@ -552,12 +571,10 @@
 
 
 def group_count(Z, B):
-    count = 2 if relaying(Z, B) else 0
-    for t in range(2):
-        for side in range(2):
-            blocks = [block_of(t, side, d, Z)[0] for d in range(1, ITERS + 1)]
-            count += len(set(blocks) - {0}) + 2 * len(set(blocks[:-1]) - {0})
-    return count
+    blocks = [[block_of(t, side, d, Z)[0] for d in range(1, ITERS + 1)] for t in range(2) for side in range(2)]
+    straight = {q for row in blocks for q in row} - {0}
+    beside = {q for row in blocks for q in row[:-1]} - {0}
+    return len(straight) + len(beside) + (2 if relaying(Z, B) else 0)
 
 
 def write_out(basis_ref, tri_ref, basis_out, tri_out, sems):
@@ -591,17 +608,14 @@
             pltpu.VMEM((RELAYED, Y, X), f32),
             pltpu.VMEM((2, n, 1, X), f32),
             dma((group_count(Z, sizes[2]),)),
-            dma((2, D)),
-            dma((2, D - 1, 2)),
+            dma((D + max(0, D - Z + H),)),
+            dma((D - 1 + max(0, D - 1 - Z + H),)),
             dma((RELAYED,)),
+            dma((1,)),
             dma((2,)),
-            dma((2,)),
-            dma((2,)),
-            dma((2,)),
-            dma((2,)),
-            dma((2,)),
-            dma((2,)),
-            dma((2,)),
+            dma((3,)),
+            dma((3,)),
+            dma((1,)),
         ],
         compiler_params=pltpu.CompilerParams(collective_id=0, has_side_effects=True),
     )(start_vector, potential)

time: 20.7 us -> 20.3 us (0.981)
  Pallas kernels: 19.9 us -> 19.5 us
    pallas_call x1, Pallas kernels: 19 us -> 18.6 us  [shards(): pl.pallas_call(functools.partial(kernel, sizes, 1.0 / (start_vector.size...]
where the time goes in v5:
time: 20.3 us; the launch traced here: 20.2 us
  Pallas kernels  19.5 us (96%)
  between operations  0.64 us (3%)
    pallas_call x1, Pallas kernels, shards(): pl.pallas_call(functools.partial(kernel, sizes, 1.0 / (start_vector.size...  18.6 us
    pallas_call x1, Pallas kernels, shards(): pl.pallas_call(write_out, out_shape=(jax.ShapeDtypeStruct(basis.shape, f3...  0.9 us

profile of v5, /device:TPU:0, one launch (start us, length us, event | category | flops | bytes accessed | tf_op | source)
XLA Modules:
  0.0 20.2 jit_solution(13018793822140093780)
XLA Ops:
  0.6 18.6 %shard_map.41 = (f32[6,8,32,128]{3,2,1,0:T(8,128)S(1)}, f32[2,5]{1,0:T(2,128)S(1)}) custom-call(f32[8,32,128]{2,1,0:T(8,128)} %x_hbm.1, f32[8,32,128]{2,1,0:T(8,128)} %pot_hbm.1), custom_call_target="tpu_custom_call" | custom-call | tf_op jit(solution)/shard_map/pallas_call | solution.py:599
  19.3 0.9 %shard_map.42 = (f32[6,8,32,128]{3,2,1,0:T(8,128)}, f32[2,5]{1,0:T(2,128)}) custom-call(f32[6,8,32,128]{3,2,1,0:T(8,128)S(1)} %get-tuple-element.4.basis_ref, f32[2,5]{1,0:T(2,128)S(1)} %get-tuple-element.5.tri_ref), custom_call_target="tpu_custom_call" | custom-call | tf_op jit(solution)/shard_map/pallas_call | solution.py:622

commit v6 on v5

--- a/solution.py
+++ b/solution.py
@@ -92,7 +92,7 @@
     return vectors[1:]
 
 
-def kernel(sizes, per_cell, x_hbm, pot_hbm, out_ref, tri_ref, cells, ext, swapped, relayed, slots,
+def kernel(sizes, per_cell, x_hbm, pot_hbm, out_ref, coeff_ref, tri_ref, cells, ext, swapped, relayed, slots,
            group_send, plane_recv, corner_recv, relay_recv, relay_send, side_sems, pair_sems, stat_sems, load_sem):
     Z, Y, X = x_hbm.shape
     S, A, B = sizes
@@ -530,6 +530,13 @@
         wait_for(relayed, relay_send.at[0])
     finish_planes()
     wait_for(swapped, pair_sems.at[2])
+    for i in range(H):
+        mine, other = slab * H + i, (1 - slab) * H + i
+        out_ref[0, mine] = cells[0, slab, D + i, inside]
+        out_ref[0, other] = cells[0, slab, first_plane + other, inside]
+        for q in range(1, D + 1):
+            out_ref[q, mine] = cells[q, slab, D + i, inside]
+            out_ref[q, other] = swapped[q - 1, i]
     stats = gathered(1, len(sums))
     scale = 1.0 / jnp.sqrt(stats[0] + EPSILON)
     inner = {}
@@ -542,21 +549,8 @@
         tri_ref[1:2, v:v + 1] = betas[v][:, 0:1]
     found = [{q: t * scale for q, t in coords.items()} for coords in found]
 
-    for half in range(2):
-        for i in range(H):
-            if half == 0:
-                z = slab * H + i
-                columns = [cells[q, slab, D + i, inside] for q in range(D + 1)]
-            else:
-                z = (1 - slab) * H + i
-                columns = [cells[0, slab, first_plane + z, inside]] + [swapped[q, i] for q in range(D)]
-            out_ref[0, z] = columns[0] * scale
-            for k, coords in enumerate(found):
-                total = None
-                for q in sorted(coords, reverse=True):
-                    term = coords[q] * columns[q]
-                    total = term if total is None else total + term
-                out_ref[k + 1, z] = total
+    for r, value in enumerate([scale] + [coords[q] for coords in found for q in range(len(coords))]):
+        coeff_ref[r:r + 1] = value
 
     wait_for(slots.at[pl.ds(0, 2), pl.ds(0, n - 1)], stat_sems.at[2])
 
@@ -577,13 +571,22 @@
     return len(straight) + len(beside) + (2 if relaying(Z, B) else 0)
 
 
-def write_out(basis_ref, tri_ref, basis_out, tri_out, sems):
-    copies = (pltpu.make_async_copy(basis_ref, basis_out, sems.at[0]),
-              pltpu.make_async_copy(tri_ref, tri_out, sems.at[1]))
-    for copy in copies:
-        copy.start()
-    for copy in copies:
-        copy.wait()
+def write_out(columns, coeff_ref, tri_ref, basis_out, tri_out, basis, sems):
+    count, Z = columns.shape[:2]
+    small = pltpu.make_async_copy(tri_ref, tri_out, sems.at[1])
+    small.start()
+    for z in range(Z):
+        held = [columns[q, z] for q in range(count)]
+        for k in range(count):
+            total = None
+            for q in reversed(range(k + 1)):
+                r = 0 if k == 0 else k * (k + 1) // 2 + q
+                term = coeff_ref[r:r + 1] * held[q]
+                total = term if total is None else total + term
+            basis[k, z] = total
+        pltpu.make_async_copy(basis.at[:, z], basis_out.at[:, z], sems.at[0]).start()
+    pltpu.make_async_copy(basis, basis_out, sems.at[0]).wait()
+    small.wait()
 
 
 def shards(sizes, start_vector, potential):
@@ -596,11 +599,12 @@
     hbm = pl.BlockSpec(memory_space=pl.ANY)
     dma = pltpu.SemaphoreType.DMA
     extended = (2, H + 2 * D, Y + 2 * T, X)
-    basis, tri = pl.pallas_call(
+    coeffs = -(-((D + 1) * (D + 2) // 2) // T) * T
+    held = pl.pallas_call(
         functools.partial(kernel, sizes, 1.0 / (start_vector.size * n)),
-        out_shape=(pltpu.VMEM((D + 1, Z, Y, X), f32), pltpu.VMEM((2, D), f32)),
+        out_shape=(pltpu.VMEM((D + 1, Z, Y, X), f32), pltpu.VMEM((coeffs, X), f32), pltpu.VMEM((2, D), f32)),
         in_specs=[hbm, hbm],
-        out_specs=(vmem, vmem),
+        out_specs=(vmem,) * 3,
         scratch_shapes=[
             pltpu.VMEM((D + 1,) + extended, f32),
             pltpu.VMEM(extended, f32),
@@ -621,11 +625,11 @@
     )(start_vector, potential)
     return tuple(pl.pallas_call(
         write_out,
-        out_shape=(jax.ShapeDtypeStruct(basis.shape, f32), jax.ShapeDtypeStruct(tri.shape, f32)),
-        in_specs=[vmem, vmem],
+        out_shape=(jax.ShapeDtypeStruct((D + 1, Z, Y, X), f32), jax.ShapeDtypeStruct((2, D), f32)),
+        in_specs=[vmem] * 3,
         out_specs=(hbm, hbm),
-        scratch_shapes=[dma((2,))],
-    )(pltpu.with_memory_space_constraint(basis, pltpu.VMEM), pltpu.with_memory_space_constraint(tri, pltpu.VMEM)))
+        scratch_shapes=[pltpu.VMEM((D + 1, Z, Y, X), f32), dma((2,))],
+    )(*(pltpu.with_memory_space_constraint(ref, pltpu.VMEM) for ref in held)))
 
 
 def solution(mesh):

time: 20.3 us -> 20.2 us (level)
  no operation moved by 1% of the time
where the time goes in v6:
time: 20.2 us; the launch traced here: 20.1 us
  Pallas kernels  19.4 us (96%)
  between operations  0.64 us (3%)
    pallas_call x1, Pallas kernels, shards(): pl.pallas_call(functools.partial(kernel, sizes, 1.0 / (start_vector.size...  18.5 us
    pallas_call x1, Pallas kernels, shards(): pl.pallas_call(write_out, out_shape=(jax.ShapeDtypeStruct((D + 1, Z, Y, X...  0.91 us

profile of v6, /device:TPU:0, one launch (start us, length us, event | category | flops | bytes accessed | tf_op | source)
XLA Modules:
  0.0 20.1 jit_solution(16291510142545739965)
XLA Ops:
  0.6 18.5 %shard_map.41 = (f32[6,8,32,128]{3,2,1,0:T(8,128)S(1)}, f32[24,128]{1,0:T(8,128)S(1)}, f32[2,5]{1,0:T(2,128)S(1)}) custom-call(f32[8,32,128]{2,1,0:T(8,128)} %x_hbm.1, f32[8,32,128]{2,1,0:T(8,128)} %pot_hbm.1), custom_call_target="tpu_custom_call" | custom-call | tf_op jit(solution)/shard_map/pallas_call | solution.py:603
  19.1 0.9 %shard_map.42 = (f32[6,8,32,128]{3,2,1,0:T(8,128)}, f32[2,5]{1,0:T(2,128)}) custom-call(f32[6,8,32,128]{3,2,1,0:T(8,128)S(1)} %get-tuple-element.5.columns, f32[24,128]{1,0:T(8,128)S(1)} %get-tuple-element.6.coeff_ref, f32[2,5]{1,0:T(2,128)S(1)} %get-tuple-element.7.tri_ref), custom_call_target="tpu_custom_call" | custom-call | tf_op jit(solution)/shard_map/pallas_call | solution.py:626

commit v7 on v6

--- a/solution.py
+++ b/solution.py
@@ -93,7 +93,7 @@
 
 
 def kernel(sizes, per_cell, x_hbm, pot_hbm, out_ref, coeff_ref, tri_ref, cells, ext, swapped, relayed, slots,
-           group_send, plane_recv, corner_recv, relay_recv, relay_send, side_sems, pair_sems, stat_sems, load_sem):
+           group_send, plane_recv, corner_recv, relay_recv, relay_send, pass_send, side_sems, pair_sems, stat_sems, load_sem):
     Z, Y, X = x_hbm.shape
     S, A, B = sizes
     n = S * A * B
@@ -218,6 +218,8 @@
             for side in range(2):
                 wanted = [(array, d) for array, d in ((VECTOR, w), (POTENTIAL, w - 1))
                           if 1 <= d <= reach(array) and plane_of(t, side, d)[0] != 0]
+                if passing(Z) and side != t:
+                    continue
                 for q in sorted({plane_of(t, side, d)[0] for _, d in wanted}, key=abs):
                     mine = [(a, d) for a, d in wanted if plane_of(t, side, d)[0] == q]
                     sign = -1 if sending else 1
@@ -271,6 +273,17 @@
             array, t, side, d, step = keys[0]
             guarded(conditions, lambda keys=keys, sem=arrival(array, t, side, d, step): wait_for(
                 lines(2 * volume(keys)), sem))
+
+    def pass_copy(t):
+        return remote(
+            cells.at[0, pl.ds(0, 2), lands(t, 1), inside], cells.at[0, pl.ds(0, 2), lands(t, D), inside],
+            pass_send.at[0], plane_recv.at[D], partner)
+
+    def each_pass(receiving, act):
+        for t in range(2):
+            if passing(Z):
+                guarded([slab == (1 - t if receiving else t), within(-1 if t == 0 else 1, pz, B)],
+                        lambda t=t: act(t))
 
     def side_copy(array, t, step):
         ref = source(array)
@@ -477,6 +490,7 @@
     for reached in range(2):
         if reached:
             take_planes(reached)
+            each_pass(False, lambda t: pass_copy(t).start())
         for e in range(1, ZE - 1):
             if depth(e) <= reached and e not in ready:
                 prepare(1, e)
@@ -513,6 +527,8 @@
     for w in range(1, D + 1):
         if w > 1:
             take_planes(w)
+        if w == D:
+            each_pass(True, lambda t: pass_copy(t).wait_recv())
         for l, e in wave(w):
             finish(l, e)
         swap_copy(w).start()
@@ -529,6 +545,7 @@
     if relays:
         wait_for(relayed, relay_send.at[0])
     finish_planes()
+    each_pass(False, lambda t: pass_copy(t).wait_send())
     wait_for(swapped, pair_sems.at[2])
     for i in range(H):
         mine, other = slab * H + i, (1 - slab) * H + i
@@ -564,8 +581,13 @@
     return B == RELAY_RING and block_of(0, 0, ITERS, Z)[0] == -1
 
 
+def passing(Z):
+    return Z - Z // 2 + 1 == ITERS
+
+
 def group_count(Z, B):
-    blocks = [[block_of(t, side, d, Z)[0] for d in range(1, ITERS + 1)] for t in range(2) for side in range(2)]
+    blocks = [[block_of(t, side, d, Z)[0] for d in range(1, ITERS + 1)] for t in range(2) for side in range(2)
+              if side == t or not passing(Z)]
     straight = {q for row in blocks for q in row} - {0}
     beside = {q for row in blocks for q in row[:-1]} - {0}
     return len(straight) + len(beside) + (2 if relaying(Z, B) else 0)
@@ -616,6 +638,7 @@
             dma((D - 1 + max(0, D - 1 - Z + H),)),
             dma((RELAYED,)),
             dma((1,)),
+            dma((1,)),
             dma((2,)),
             dma((3,)),
             dma((3,)),

time: 20.2 us -> 19.9 us (0.985)
    pallas_call x1, Pallas kernels: 18.5 us -> 18.2 us  [shards(): pl.pallas_call(functools.partial(kernel, sizes, 1.0 / (start_vector.size...]
where the time goes in v7:
time: 19.9 us; the launch traced here: 19.8 us
  Pallas kernels  19.2 us (96%)
  between operations  0.64 us (3%)
    pallas_call x1, Pallas kernels, shards(): pl.pallas_call(functools.partial(kernel, sizes, 1.0 / (start_vector.size...  18.2 us
    pallas_call x1, Pallas kernels, shards(): pl.pallas_call(write_out, out_shape=(jax.ShapeDtypeStruct((D + 1, Z, Y, X...  0.91 us

profile of v7, /device:TPU:0, one launch (start us, length us, event | category | flops | bytes accessed | tf_op | source)
XLA Modules:
  0.0 19.8 jit_solution(12445246232136735094)
XLA Ops:
  0.6 18.2 %shard_map.41 = (f32[6,8,32,128]{3,2,1,0:T(8,128)S(1)}, f32[24,128]{1,0:T(8,128)S(1)}, f32[2,5]{1,0:T(2,128)S(1)}) custom-call(f32[8,32,128]{2,1,0:T(8,128)} %x_hbm.1, f32[8,32,128]{2,1,0:T(8,128)} %pot_hbm.1), custom_call_target="tpu_custom_call" | custom-call | tf_op jit(solution)/shard_map/pallas_call | solution.py:625
  18.9 0.9 %shard_map.42 = (f32[6,8,32,128]{3,2,1,0:T(8,128)}, f32[2,5]{1,0:T(2,128)}) custom-call(f32[6,8,32,128]{3,2,1,0:T(8,128)S(1)} %get-tuple-element.5.columns, f32[24,128]{1,0:T(8,128)S(1)} %get-tuple-element.6.coeff_ref, f32[2,5]{1,0:T(2,128)S(1)} %get-tuple-element.7.tri_ref), custom_call_target="tpu_custom_call" | custom-call | tf_op jit(solution)/shard_map/pallas_call | solution.py:649

commit v8 on v7

--- a/solution.py
+++ b/solution.py
@@ -93,7 +93,7 @@
 
 
 def kernel(sizes, per_cell, x_hbm, pot_hbm, out_ref, coeff_ref, tri_ref, cells, ext, swapped, relayed, slots,
-           group_send, plane_recv, corner_recv, relay_recv, relay_send, pass_send, side_sems, pair_sems, stat_sems, load_sem):
+           group_send, plane_recv, corner_recv, relay_recv, relay_send, pass_send, side_sems, pair_sems, stat_sems):
     Z, Y, X = x_hbm.shape
     S, A, B = sizes
     n = S * A * B
@@ -197,7 +197,7 @@
         array, d = relays[k]
         z = plane_of(t, t, d)[1]
         return remote(source(array).at[slab, z + first_plane, inside], relayed.at[k],
-                      relay_send.at[0], relay_recv.at[k], (slab, py, B - 1 if t == 0 else 0))
+                      relay_send.at[0], relay_recv.at[2 * k // RELAYED], (slab, py, B - 1 if t == 0 else 0))
 
     def onward_copy(k, t):
         array, d = relays[k]
@@ -325,14 +325,14 @@
     def fold(value):
         return jnp.sum(value.reshape(value.shape[0] // T, T, X), axis=0)
 
-    def share(p, sums):
-        lines = [jnp.sum(v, axis=0, keepdims=True) for v in sums]
-        height = -(-len(lines) // T) * T
-        lines = lines + [jnp.zeros((1, X), jnp.float32)] * (height - len(lines))
-        totals = jnp.sum(jnp.concatenate(lines, axis=0), axis=1, keepdims=True)
-        at = lax.broadcasted_iota(jnp.int32, (height, X), 0)
+    def packed(sums, first=0):
+        lines_ = [jnp.sum(v, axis=0, keepdims=True) for v in sums]
+        height = -(-len(lines_) // T) * T
+        lines_ = lines_ + [jnp.zeros((1, X), jnp.float32)] * (height - len(lines_))
+        totals = jnp.sum(jnp.concatenate(lines_, axis=0), axis=1, keepdims=True)
+        at = lax.broadcasted_iota(jnp.int32, (height, X), 0) + first
         lanes = lax.broadcasted_iota(jnp.int32, (height, X), 1)
-        slots[p, me] = jnp.sum(jnp.where(at == lanes, totals, 0.0), axis=0, keepdims=True)
+        return jnp.sum(jnp.where(at == lanes, totals, 0.0), axis=0, keepdims=True)
 
     def gathered(p, count):
         wait_for(slots.at[p, pl.ds(0, n - 1)], stat_sems.at[p])
@@ -342,7 +342,7 @@
     barrier = pltpu.get_barrier_semaphore()
     to_others(lambda t: pl.semaphore_signal(barrier, inc=1, device_id=t, device_id_type=MESH))
     loads = [pltpu.make_async_copy(
-        hbm, source(array).at[slab, pl.ds(first_plane, Z), inside], load_sem.at[0])
+        hbm, source(array).at[slab, pl.ds(first_plane, Z), inside], pair_sems.at[0])
         for array, hbm in ((VECTOR, x_hbm), (POTENTIAL, pot_hbm))]
     for load in loads:
         load.start()
@@ -364,7 +364,7 @@
                 for core in range(2):
                     for e in range(ZE):
                         ref[core, e, at:at + T] = jnp.zeros((T, X), jnp.float32)
-    wait_for(lines(2 * Z * Y), load_sem.at[0])
+    wait_for(lines(2 * Z * Y), pair_sems.at[0])
 
     def rough():
         lane = lax.broadcasted_iota(jnp.int32, (Y, X), 1)
@@ -392,7 +392,7 @@
                 sums[i] = sums[i] + fold(u * v)
         return sums
 
-    share(0, rough())
+    slots[0, me] = packed(rough())
     pl.semaphore_wait(barrier, n - 1)
 
     each_relay((1, 2), lambda k, t: relay_copy(k, t).start())
@@ -405,7 +405,9 @@
         send_planes(w)
 
     def forward(k, t):
-        relay_copy(k, t).wait_recv()
+        part = [i for i in range(RELAYED) if 2 * i // RELAYED == 2 * k // RELAYED]
+        if k == part[0]:
+            wait_for(relayed.at[pl.ds(k, len(part))], relay_recv.at[2 * k // RELAYED])
         onward_copy(k, t).start()
 
     each_relay((B - 1, 0), forward)
@@ -533,12 +535,11 @@
             finish(l, e)
         swap_copy(w).start()
         if w == D - 1:
-            sums = measure(early, held)
+            slots[1, me] = packed(measure(early, held))
             last = measure(late, done)
         if w < D:
             prepare_all(wave(w + 1))
-    sums = sums + measure(late, [e for e in held if e not in done], last)
-    share(1, sums)
+    slots[1, me] = slots[1, me] + packed(measure(late, [e for e in held if e not in done], last), len(early))
     to_others(lambda target: stat_copy(1, target).start())
     wait_for(lines((2 * Z + D * H) * Y), pair_sems.at[0])
     wait_sides(side_sems.at[0])
@@ -554,7 +555,7 @@
         for q in range(1, D + 1):
             out_ref[q, mine] = cells[q, slab, D + i, inside]
             out_ref[q, other] = swapped[q - 1, i]
-    stats = gathered(1, len(sums))
+    stats = gathered(1, len(early) + len(late))
     scale = 1.0 / jnp.sqrt(stats[0] + EPSILON)
     inner = {}
     for (k, l), value in zip(early + late, stats):
@@ -636,13 +637,12 @@
             dma((group_count(Z, sizes[2]),)),
             dma((D + max(0, D - Z + H),)),
             dma((D - 1 + max(0, D - 1 - Z + H),)),
-            dma((RELAYED,)),
+            dma((2,)),
             dma((1,)),
             dma((1,)),
             dma((2,)),
             dma((3,)),
             dma((3,)),
-            dma((1,)),
         ],
         compiler_params=pltpu.CompilerParams(collective_id=0, has_side_effects=True),
     )(start_vector, potential)

time: 19.9 us -> 20 us (level)
  no operation moved by 1% of the time
where the time goes in v8:
time: 20 us; the launch traced here: 19.8 us
  Pallas kernels  19.2 us (96%)
  between operations  0.64 us (3%)
    pallas_call x1, Pallas kernels, shards(): pl.pallas_call(functools.partial(kernel, sizes, 1.0 / (start_vector.size...  18.3 us
    pallas_call x1, Pallas kernels, shards(): pl.pallas_call(write_out, out_shape=(jax.ShapeDtypeStruct((D + 1, Z, Y, X...  0.91 us

profile of v8, /device:TPU:0, one launch (start us, length us, event | category | flops | bytes accessed | tf_op | source)
XLA Modules:
  0.0 19.8 jit_solution(14710060062502996271)
XLA Ops:
  0.6 18.3 %shard_map.41 = (f32[6,8,32,128]{3,2,1,0:T(8,128)S(1)}, f32[24,128]{1,0:T(8,128)S(1)}, f32[2,5]{1,0:T(2,128)S(1)}) custom-call(f32[8,32,128]{2,1,0:T(8,128)} %x_hbm.1, f32[8,32,128]{2,1,0:T(8,128)} %pot_hbm.1), custom_call_target="tpu_custom_call" | custom-call | tf_op jit(solution)/shard_map/pallas_call | solution.py:626
  18.9 0.9 %shard_map.42 = (f32[6,8,32,128]{3,2,1,0:T(8,128)}, f32[2,5]{1,0:T(2,128)}) custom-call(f32[6,8,32,128]{3,2,1,0:T(8,128)S(1)} %get-tuple-element.5.columns, f32[24,128]{1,0:T(8,128)S(1)} %get-tuple-element.6.coeff_ref, f32[2,5]{1,0:T(2,128)S(1)} %get-tuple-element.7.tri_ref), custom_call_target="tpu_custom_call" | custom-call | tf_op jit(solution)/shard_map/pallas_call | solution.py:649

commit v9 on v8

--- a/solution.py
+++ b/solution.py
@@ -19,7 +19,7 @@
 LEAST_SHIFT, MOST_SHIFT = 0.5, 16.5
 VECTOR, POTENTIAL = 0, 1
 RELAY_RING, RELAYED = 4, 5
-CHUNK = 3
+CHUNK = 2
 
 
 def times(coeff, columns):
@@ -395,9 +395,9 @@
     slots[0, me] = packed(rough())
     pl.semaphore_wait(barrier, n - 1)
 
+    to_others(lambda target: stat_copy(0, target).start())
     each_relay((1, 2), lambda k, t: relay_copy(k, t).start())
     send_planes(1)
-    to_others(lambda target: stat_copy(0, target).start())
     for array in (VECTOR, POTENTIAL):
         near_copy(array).start()
     send_sides()

time: 20 us -> 20 us (level)
  no operation moved by 1% of the time
where the time goes in v9:
time: 20 us; the launch traced here: 19.8 us
  Pallas kernels  19.2 us (96%)
  between operations  0.64 us (3%)
    pallas_call x1, Pallas kernels, shards(): pl.pallas_call(functools.partial(kernel, sizes, 1.0 / (start_vector.size...  18.3 us
    pallas_call x1, Pallas kernels, shards(): pl.pallas_call(write_out, out_shape=(jax.ShapeDtypeStruct((D + 1, Z, Y, X...  0.91 us

profile of v9, /device:TPU:0, one launch (start us, length us, event | category | flops | bytes accessed | tf_op | source)
XLA Modules:
  0.0 19.8 jit_solution(15812172848453318341)
XLA Ops:
  0.6 18.3 %shard_map.41 = (f32[6,8,32,128]{3,2,1,0:T(8,128)S(1)}, f32[24,128]{1,0:T(8,128)S(1)}, f32[2,5]{1,0:T(2,128)S(1)}) custom-call(f32[8,32,128]{2,1,0:T(8,128)} %x_hbm.1, f32[8,32,128]{2,1,0:T(8,128)} %pot_hbm.1), custom_call_target="tpu_custom_call" | custom-call | tf_op jit(solution)/shard_map/pallas_call | solution.py:626
  18.9 0.9 %shard_map.42 = (f32[6,8,32,128]{3,2,1,0:T(8,128)}, f32[2,5]{1,0:T(2,128)}) custom-call(f32[6,8,32,128]{3,2,1,0:T(8,128)S(1)} %get-tuple-element.5.columns, f32[24,128]{1,0:T(8,128)S(1)} %get-tuple-element.6.coeff_ref, f32[2,5]{1,0:T(2,128)S(1)} %get-tuple-element.7.tri_ref), custom_call_target="tpu_custom_call" | custom-call | tf_op jit(solution)/shard_map/pallas_call | solution.py:649
